TPU v7x, 32 devices: a whole 2x2x4 slice. The times are simulated.
32 devices in a mesh: dp: 16 (over z, x, core), tp: 2 (over y).
Axes of the slice: x: 2, y: 2, z: 4, core: 2. Of those that a mesh axis runs over, the one named last changes fastest.
Arguments:
- queries: bfloat16 [128, 8192], P('dp', 'tp'), may hold values from -5 to 5
- prefix_kv: bfloat16 [2, 32768, 1024], P(None, 'dp', 'tp'), may hold values from -5 to 5
- cache_kv: bfloat16 [2, 1024, 64, 1024], P(None, 'dp', None, 'tp'), may hold values from -5 to 5
- lengths: int32 [128], P('dp'), may hold values from 1 to 512, as said below
- page_table: int32 [16, 64], P('dp'), may hold values from 0 to 63, each once within a row
- owner: int32 [16], replicated, may hold values from 0 to 15, as said below
- readers: int32 [8], replicated, may hold values from 0 to 15, as said below
- w_out: bfloat16 [8192, 4096], P('tp'), may hold values from -0.5 to 0.5
Outputs:
- projected: bfloat16 [128, 4096], P('dp', 'tp')
Inputs may be any that keep to these rules, and one draw needn't show every extreme that they name: `lengths`: at most 512, reached by some request in every draw. `page_table`: each row holds every page id of its replica once. `owner`: every replica index once. `readers`: 8 distinct replica indices, none of them owner[0].
All inputs are finite; a program needn't handle non-finite values.
Results may differ from a plain program's by a relative error of at most 0.0051.
Values may be sent and summed in bfloat16 or wider, within the bound.
No kernel may reach another device: no remote copies, remote signals or barrier semaphores. Data moves between devices by JAX's collectives and lax.ppermute only.
A program may use at most 128 MiB of HBM per device.

v0:
```python
import jax
import jax.numpy as jnp
from jax import lax
from jax.sharding import PartitionSpec as P

HD = 128
PREFIX = 2048
PAGE = 64


def from_root(block, axis, holder):
    block = jnp.where(lax.axis_index(axis) == holder, block, jnp.zeros_like(block))
    return lax.psum(block, axis)


def shards(queries, prefix_kv, cache_kv, lengths, page_table, owner, readers, w_out):
    rows = queries.shape[0]
    heads_here = queries.shape[1] // HD
    groups_here = prefix_kv.shape[2] // HD
    group = heads_here // groups_here
    maxpages = page_table.shape[1] // rows
    scale = 1.0 / HD**0.5
    replica_id = lax.axis_index("dp")
    matches = readers == replica_id
    is_reader = jnp.any(matches)
    query = queries.reshape(rows, groups_here, group, HD)
    pages = page_table[0].reshape(rows, maxpages)
    resident = cache_kv[:, pages].reshape(2, rows, maxpages * PAGE, groups_here, HD)
    s_res = (
        jnp.einsum("bkgd,btkd->bkgt", query, resident[0], preferred_element_type=jnp.float32)
        * scale
    )
    inside = jnp.arange(maxpages * PAGE, dtype=jnp.int32)[None, :] < lengths[:, None]
    s_res = jnp.where(inside[:, None, None, :], s_res, -jnp.inf)
    top_res = jnp.max(s_res, axis=-1)
    shared = from_root(prefix_kv, "dp", owner[0])
    shared = shared.reshape(2, PREFIX, groups_here, HD)
    s_pre = (
        jnp.einsum("bkgd,tkd->bkgt", query, shared[0], preferred_element_type=jnp.float32) * scale
    )
    s_pre = jnp.where(is_reader, s_pre, -jnp.inf)
    top = jnp.maximum(top_res, jnp.max(s_pre, axis=-1))
    e_pre = jnp.exp(s_pre - top[..., None])
    den_pre = jnp.sum(e_pre, axis=-1)
    num_pre = jnp.einsum(
        "bkgt,tkd->bkgd", e_pre.astype(jnp.bfloat16), shared[1], preferred_element_type=jnp.float32
    )
    e_res = jnp.exp(s_res - top[..., None])
    den = jnp.sum(e_res, axis=-1) + den_pre
    num = (
        jnp.einsum(
            "bkgt,btkd->bkgd",
            e_res.astype(jnp.bfloat16),
            resident[1],
            preferred_element_type=jnp.float32,
        )
        + num_pre
    )
    attn = (num / den[..., None]).astype(jnp.bfloat16).reshape(rows, heads_here * HD)
    partial_out = jnp.dot(attn, w_out, preferred_element_type=jnp.float32)
    return lax.psum_scatter(partial_out, "tp", scatter_dimension=1, tiled=True).astype(jnp.bfloat16)


def solution(mesh):
    placed = (
        P("dp", "tp"),
        P(None, "dp", "tp"),
        P(None, "dp", None, "tp"),
        P("dp"),
        P("dp", None),
        P(),
        P(),
        P("tp", None),
    )
    return jax.shard_map(
        shards, mesh=mesh, in_specs=placed, out_specs=P("dp", "tp"), check_vma=False
    )
```

profile of v0, /device:TPU:0, one launch (start us, length us, event | category | flops | bytes accessed | tf_op | source)
XLA Modules:
  0.0 169.8 jit_solution(3543943797238517936)
XLA Ops:
  6.5 6.4 %copy.49 = bf16[2,2048,512]{1,2,0:T(8,128)(2,1)} copy(bf16[2,2048,512]{2,1,0:T(8,128)(2,1)} %param.9) | data formatting | bytes 8388608 | tf_op args[1]
  12.9 2.3 %broadcast_select_fusion = bf16[2,2048,512]{1,2,0:T(8,128)(2,1)} fusion(bf16[2,2048,512]{1,2,0:T(8,128)(2,1)} %copy.49, pred[]{:T(512)S(6)} %eq.11), kind=kLoop, calls=%fused_computation.6 | loop fusion | flops 2097152 | bytes 8388609 | tf_op jit(solution)/shard_map/jit(_where)/select_n | solution.py:12
  15.3 0.5 broadcast.41
  15.9 0.7 reduce.3
  16.5 0.1 reshape_squeeze.3
  16.6 0.1 reshape.75
  16.7 9.0 %gather_fusion = bf16[64,2,64,512]{3,2,1,0:T(8,128)(2,1)} fusion(bf16[2,64,64,512]{3,2,1,0:T(8,128)(2,1)} %param.10, s32[1024]{0:T(1024)S(1)} %pad_clamp_fusion), kind=kCustom, calls=%fused_computation | custom fusion | bytes 16777472 | tf_op jit(solution)/shard_map/gather | solution.py:28
  25.7 7.8 %copy.101 = bf16[8,8,2,64,512]{4,3,1,0,2:T(8,128)(2,1)} copy(bf16[8,8,2,64,512]{4,3,2,1,0:T(8,128)(2,1)} %bitcast.38) | data formatting | bytes 16777216 | tf_op jit(solution)/shard_map/gather | solution.py:28
  33.5 6.1 %fusion.39 = (bf16[1,8,8,64,512]{4,3,2,1,0:T(8,128)(2,1)}, bf16[1,8,8,64,512]{4,3,2,1,0:T(8,128)(2,1)}) fusion(bf16[2,8,8,64,512]{4,3,2,1,0:T(8,128)(2,1)} %bitcast.39), kind=kLoop, calls=%fused_computation.37 | loop fusion | bytes 16777216 | tf_op jit(solution)/shard_map/slice | solution.py:54
  39.6 7.0 %squeeze.15 = bf16[8,512,4,128]{3,2,1,0:T(4,128)(2,1)} reshape(bf16[1,8,8,64,512]{4,3,2,1,0:T(8,128)(2,1)} %get-tuple-element.6) | data formatting | bytes 8388608 | tf_op jit(solution)/shard_map/squeeze | solution.py:30
  46.6 7.0 %squeeze.18 = bf16[8,512,4,128]{3,2,1,0:T(4,128)(2,1)} reshape(bf16[1,8,8,64,512]{4,3,2,1,0:T(8,128)(2,1)} %get-tuple-element.5) | data formatting | bytes 8388608 | tf_op jit(solution)/shard_map/squeeze | solution.py:54
  53.6 0.6 compare_reduce_fusion
  54.3 3.5 %fusion.42 = (f32[8,4,8]{2,1,0:T(4,128)S(1)}, f32[8,4,8,512]{3,2,1,0:T(8,128)S(1)}) fusion(bf16[8,4,8,128]{3,0,2,1:T(8,128)(2,1)S(1)} %bitcast.36, bf16[8,512,4,128]{3,2,1,0:T(4,128)(2,1)} %squeeze.15, pred[8,512]{1,0:T(8,128)(4,1)S(1)} %iota_compare_fusion), kind=kOutput, calls=%fused_computation.40 | convolution fusion | flops 33947392 | bytes 4789248 | tf_op jit(solution)/shard_map/bkgd,btkd->bkgt/dot_general | solution.py:30
  57.9 73.5 %all-reduce.2.cloned.1.call-done = bf16[2,2048,512]{1,2,0:T(8,128)(2,1)} async-done(((bf16[2,2048,512]{1,2,0:T(8,128)(2,1)}), bf16[2,2048,512]{1,2,0:T(8,128)(2,1)}) %all-reduce.2.cloned.1.call-update) | async-done | bytes 4194320 | tf_op jit(solution)/shard_map/psum | solution.py:13
  131.4 2.7 %fusion.40 = (bf16[1,2048,512]{1,2,0:T(8,128)(2,1)S(1)}, bf16[1,2048,512]{1,2,0:T(8,128)(2,1)S(1)}) fusion(bf16[2,2048,512]{1,2,0:T(8,128)(2,1)} %all-reduce.2.cloned.1.call-done), kind=kLoop, calls=%fused_computation.38 | loop fusion | bytes 8388608 | tf_op jit(solution)/shard_map/slice | solution.py:39
  134.1 1.2 fusion.41
  135.4 0.5 fusion.6
  135.8 0.8 convolution_bitcast_fusion
  136.7 0.3 fusion.30
  136.9 0.6 copy-done.1
  137.5 0.8 fusion.26
  138.3 13.5 %fusion.34 = f32[8,4096]{1,0:T(8,128)} fusion(bf16[4096,4096]{1,0:T(8,128)(2,1)} %param.15, bf16[1,8,32,128]{3,2,1,0:T(8,128)(2,1)S(1)} %fusion.26), kind=kOutput, calls=%fused_computation.26 | convolution fusion | flops 268435456 | bytes 33751040 | tf_op jit(solution)/shard_map/dot_general | solution.py:60
  151.8 9.7 %reduce-scatter.2.cloned.1.call-done = f32[8,2048]{1,0:T(8,128)} async-done(((f32[8,4096]{1,0:T(8,128)}), f32[8,2048]{1,0:T(8,128)}) %reduce-scatter.2.cloned.1.call-update) | async-done | bytes 65552 | tf_op jit(solution)/shard_map/reduce_scatter | solution.py:61
  161.5 1.5 convert_element_type.15
  (21 shorter events, 0.3 us)
Async XLA Ops:
  6.5 47.8 %copy-start = (bf16[8,4096]{1,0:T(8,128)(2,1)S(1)}, bf16[8,4096]{1,0:T(8,128)(2,1)}, u32[]{:S(2)}) copy-start(bf16[8,4096]{1,0:T(8,128)(2,1)} %param.8) | copy-start | bytes 196612
  6.5 124.8 %all-reduce.2.cloned.1.call-start = ((), (), s32[]{:S(2)}) async-start(), calls=%async_computation.1 | async-start | bytes 8388608 | tf_op jit(solution)/shard_map/psum | solution.py:13
  6.5 6.4 %copy-start.3 = (s32[16]{0:T(128)S(1)}, s32[16]{0:T(128)}, u32[]{:S(2)}) copy-start(s32[16]{0:T(128)} %param.13) | copy-start | bytes 196
  15.2 0.7 copy-start.4
  15.2 146.2 %reduce-scatter.2.cloned.1.call-start = ((), (), s32[]{:S(2)}) async-start(), calls=%async_computation.2 | async-start | bytes 196608 | tf_op jit(solution)/shard_map/reduce_scatter | solution.py:61
  46.6 7.0 %copy-start.5 = (s32[8]{0:T(128)S(1)}, s32[8]{0:T(128)}, u32[]{:S(2)}) copy-start(s32[8]{0:T(128)} %param.14) | copy-start | bytes 100
  46.6 7.6 %copy-start.2 = (s32[8]{0:T(128)S(1)}, s32[8]{0:T(128)}, u32[]{:S(2)}) copy-start(s32[8]{0:T(128)} %param.11) | copy-start | bytes 100
  135.4 2.2 %copy-start.1 = (bf16[8,512,4,128]{3,2,1,0:T(4,128)(2,1)S(1)}, bf16[8,512,4,128]{3,2,1,0:T(4,128)(2,1)}, u32[]{:S(2)}) copy-start(bf16[8,512,4,128]{3,2,1,0:T(4,128)(2,1)} %squeeze.18) | copy-start | bytes 12582916
Sparse Core Ops, SparseCore 0:
  15.3 115.9 all-reduce.1
  151.9 9.4 reduce-scatter.1
where the time goes:
time: 171 us; the launch traced here: 170 us
  waiting for transfers between devices  83.2 us (49%)
  local copies, waits for them, and re-layouts  47.4 us (28%)
  matrix products  19.8 us (12%)
  between operations  13.5 us (8%)
  other arithmetic  5.81 us (3%)
    psum x1, waiting for transfers between devices, from_root(): return lax.psum(block, axis)  73.5 us
    gather x2, local copies, waits for them, and re-layouts, shards(): cache_kv[:, pages].reshape(2, rows, maxpages * PAGE, groups_here, HD)  16.8 us
    dot_general x1, matrix products, shards(): partial_out = jnp.dot(attn, w_out, preferred_element_type=jnp.float32)  13.5 us
    reduce_scatter x1, waiting for transfers between devices, shards(): lax.psum_scatter(partial_out, 'tp', scatter_dimension=1, tiled=True)  9.65 us
    unnamed x14, local copies, waits for them, and re-layouts  7.57 us
    squeeze x1, local copies, waits for them, and re-layouts, shards(): resident[1]  6.99 us
    squeeze x1, local copies, waits for them, and re-layouts, shards(): resident[0]  6.99 us
    slice x1, local copies, waits for them, and re-layouts, shards(): resident[1]  6.1 us
  transfers between devices with their start and end apart: 2, of which 2 were waited for; matrix products, arithmetic and copies ran while one was open for 25% of the time, Pallas kernels for 0%

commit v1 on v0

v1 whole, which is shorter than its diff:
```python
import functools

import jax
import jax.numpy as jnp
from jax import lax
from jax.experimental import pallas as pl
from jax.experimental.pallas import tpu as pltpu
from jax.sharding import PartitionSpec as P


HD = 128
PAGE = 64
LOG2E = 1.4426950408889634
VMEM = pltpu.VMEM
SMEM = pltpu.SMEM


def vmem_spec():
    return pl.BlockSpec(memory_space=VMEM)


def smem_spec():
    return pl.BlockSpec(memory_space=SMEM)


def hbm_spec():
    return pl.BlockSpec(memory_space=pltpu.HBM)


def in_hbm(x):
    return pltpu.with_memory_space_constraint(x, pltpu.HBM)


def place():
    return lax.axis_index("dp").astype(jnp.int32)


def split_kernel(half, q_ref, mine, other):
    core = lax.rem(place(), 2)
    mine[...] = q_ref[:, pl.ds(pl.multiple_of(core * half, 128), half)]
    other[...] = q_ref[:, pl.ds(pl.multiple_of((1 - core) * half, 128), half)]


def pair_kernel(mine, got, after, out):
    out[0] = mine[...]
    out[1] = got[...]


def share_kernel(cols, kv, after, out, sem):
    side = 1 - lax.rem(place(), 2) if kv.shape[2] > cols else 0
    copy = pltpu.make_async_copy(kv.at[:, :, pl.ds(pl.multiple_of(side * cols, 128), cols)], out, sem)
    copy.start()
    copy.wait()


def w_copies(plan, first, w, outs, sems):
    n_tp, chunk, width = plan
    per_chunk = chunk // width
    my_tp = lax.axis_index("tp").astype(jnp.int32)
    copies = []
    for i, out in enumerate(outs):
        which, block = divmod(first + i, per_chunk)
        col = jnp.bitwise_xor(my_tp, (which + 1) % n_tp) * chunk + block * width
        copies.append(pltpu.make_async_copy(w.at[:, pl.ds(pl.multiple_of(col, 128), width)], out, sems.at[i]))
    return copies


def choose_kernel(chips, owner, *refs):
    parts, near, far = refs[:chips], refs[chips], refs[chips + 1]
    source = jnp.bitwise_xor(place() // 2, owner[0] // 2)
    for d in range(chips):

        @pl.when(source == d)
        def _():
            near[...] = parts[d][0]
            far[...] = parts[d][1]


def resident_kernel(rows, groups, group, maxpages, plan, count, table, lengths, q_ref, cache, kv, w, *refs):
    out, lse_out, own = refs[:3]
    kbuf, vbuf, sems, own_sem, w_sems = refs[3 + count :]
    length = maxpages * PAGE
    scale = 1.0 / HD**0.5
    for kind, buf in ((0, kbuf), (1, vbuf)):
        for b in range(rows):
            for t in range(maxpages):
                pltpu.make_async_copy(
                    cache.at[kind, table[b * maxpages + t]], buf.at[b, t], sems.at[kind, b]
                ).start()
    cols = own.shape[2]
    part = lax.rem(place(), 2) if kv.shape[2] > cols else 0
    own_copy = pltpu.make_async_copy(kv.at[:, :, pl.ds(pl.multiple_of(part * cols, 128), cols)], own, own_sem)
    own_copy.start()
    w_parts = w_copies(plan, 0, w, refs[3 : 3 + count], w_sems)
    for copy in w_parts:
        copy.start()
    m_rows = group * rows
    row_b = lax.rem(lax.broadcasted_iota(jnp.int32, (m_rows, 1), 0), rows)
    lens = jnp.zeros((m_rows, 1), jnp.int32)
    for b in range(rows):
        lens = jnp.where(row_b == b, lengths[b], lens)
    inside = lax.broadcasted_iota(jnp.int32, (m_rows, length), 1) < lens
    for b in range(rows):
        pltpu.make_async_copy(cache.at[0, pl.ds(0, maxpages)], kbuf.at[b], sems.at[0, b]).wait()
    probs = []
    stats = []
    for g in range(groups):
        qs = [q_ref[:, (g * group + h) * HD : (g * group + h + 1) * HD].astype(jnp.float32) for h in range(group)]
        qg = jnp.concatenate(qs, axis=0).astype(jnp.bfloat16)
        s = None
        for b in range(rows):
            kb = kbuf[b, :, :, g * HD : (g + 1) * HD].reshape(length, HD)
            sb = lax.dot_general(qg, kb, (((1,), (1,)), ((), ())), preferred_element_type=jnp.float32)
            s = sb if s is None else jnp.where(row_b == b, sb, s)
        s = jnp.where(inside, s, -jnp.inf)
        top = jnp.max(s, axis=1, keepdims=True)
        p = jnp.exp2((s - top) * (scale * LOG2E))
        den = jnp.sum(p, axis=1, keepdims=True)
        probs.append(p.astype(jnp.bfloat16))
        stats.append((1.0 / den, top * scale + jnp.log(den)))
    for b in range(rows):
        pltpu.make_async_copy(cache.at[1, pl.ds(0, maxpages)], vbuf.at[b], sems.at[1, b]).wait()
    half_heads = groups * group // 2
    lane = lax.broadcasted_iota(jnp.int32, (rows, 128), 1)
    lse = [jnp.zeros((rows, 128), jnp.float32) for _ in range(2)]
    for g in range(groups):
        o = None
        for b in range(rows):
            vb = vbuf[b, :, :, g * HD : (g + 1) * HD].reshape(length, HD)
            ob = jnp.dot(probs[g], vb, preferred_element_type=jnp.float32)
            o = ob if o is None else jnp.where(row_b == b, ob, o)
        inv, lg = stats[g]
        o = o * inv
        for h in range(group):
            side, hh = divmod(g * group + h, half_heads)
            out[side, :, hh * HD : (hh + 1) * HD] = o[h * rows : (h + 1) * rows, :]
            lse[side] = jnp.where(lane == hh, lg[h * rows : (h + 1) * rows, :], lse[side])
    for side in range(2):
        lse_out[side] = lse[side]
    own_copy.wait()
    for copy in w_parts:
        copy.wait()


def prefix_kernel(chips, rows, groups, group, n_readers, block, plan, first_w, count, owner_ref, readers, *refs):
    q_refs = refs[:chips]
    own_kv, mate_kv, w = refs[chips : chips + 3]
    outs, w_dst = refs[chips + 3 : 2 * chips + 3], refs[2 * chips + 3 : 2 * chips + 3 + count]
    q_all, q_rows, o_rows, lse_rows, o_all, w_sems = refs[2 * chips + 3 + count :]
    w_parts = w_copies(plan, first_w, w, w_dst, w_sems)
    for copy in w_parts:
        copy.start()
    me, owner = place(), owner_ref[0]
    scale = 1.0 / HD**0.5
    half = groups * group * HD

    @pl.when(me // 2 == owner // 2)
    def _():
        for d in range(chips):
            for s in range(2):
                q_all[2 * d + s] = q_refs[d][s].astype(jnp.float32)
        for j in range(n_readers):
            slot = jnp.bitwise_xor(readers[j], me)
            x = q_all[slot]
            for g in range(groups):
                for h in range(group):
                    first = (h * n_readers + j) * rows
                    col = (g * group + h) * HD
                    q_rows[g, first : first + rows, :] = x[:, col : col + HD]
        total = group * n_readers * rows
        blocks = total // block

        def attend(kv):
            for g in range(groups):

                @pl.loop(0, blocks)
                def _(i):
                    part = pl.ds(pl.multiple_of(i * block, block), block)
                    q = q_rows[g, part, :].astype(jnp.bfloat16)
                    keys = kv[0, :, g * HD : (g + 1) * HD]
                    s = lax.dot_general(q, keys, (((1,), (1,)), ((), ())), preferred_element_type=jnp.float32)
                    top = jnp.max(s, axis=1, keepdims=True)
                    p = jnp.exp2((s - top) * (scale * LOG2E))
                    den = jnp.sum(p, axis=1, keepdims=True)
                    values = kv[1, :, g * HD : (g + 1) * HD]
                    o = jnp.dot(p.astype(jnp.bfloat16), values, preferred_element_type=jnp.float32)
                    o_rows[g, part, :] = o * (1.0 / den)
                    lse_rows[g, part, :] = jnp.broadcast_to(top * scale + jnp.log(den), (block, 128))

        @pl.when(me == owner)
        def _():
            attend(own_kv)

        @pl.when(me != owner)
        def _():
            attend(mate_kv)

        lane = lax.broadcasted_iota(jnp.int32, (rows, 128), 1)
        heads = groups * group
        for j in range(n_readers):
            slot = jnp.bitwise_xor(readers[j], me)
            stat = jnp.zeros((rows, 128), jnp.float32)
            for g in range(groups):
                for h in range(group):
                    first = (h * n_readers + j) * rows
                    hh = g * group + h
                    o_all[slot, :, hh * HD : (hh + 1) * HD] = o_rows[g, first : first + rows, :]
                    val = lse_rows[g, first : first + rows, :]
                    top = val.astype(jnp.bfloat16).astype(jnp.float32)
                    rest = val - top
                    mid = rest.astype(jnp.bfloat16).astype(jnp.float32)
                    stat = jnp.where(lane == hh, top, stat)
                    stat = jnp.where(lane == heads + hh, mid, stat)
                    stat = jnp.where(lane == 2 * heads + hh, rest - mid, stat)
            o_all[slot, :, half:] = stat
        for d in range(chips):
            for s in range(2):
                outs[d][s] = o_all[2 * d + s].astype(jnp.bfloat16)

    for copy in w_parts:
        copy.wait()


def project(attn, w, outs, first, width):
    per_chunk = outs[0].shape[1] // width
    for i, out in enumerate(outs):
        for j in range(per_chunk):
            block = w[first + i * per_chunk + j]
            out[:, j * width : (j + 1) * width] = jnp.dot(attn, block[...], preferred_element_type=jnp.float32)


def away_kernel(heads, plan, loaded, later, readers, near, far, res, res_lse, w_hbm, *refs):
    n_tp, chunk, width = plan
    w, outs, attn, w_dst, w_sems = (
        refs[:loaded],
        refs[loaded : loaded + n_tp - 1],
        refs[loaded + n_tp - 1],
        refs[loaded + n_tp : loaded + n_tp + later],
        refs[-1],
    )
    copies = w_copies(plan, n_tp * (chunk // width) - later, w_hbm, w_dst, w_sems)
    for copy in copies:
        copy.start()
    me = place()
    core = lax.rem(me, 2)
    is_reader = jnp.int32(0)
    for j in range(readers.shape[0]):
        is_reader = jnp.where(readers[j] == me, 1, is_reader)
    half = heads * HD
    for side in range(2):
        mine = core == side
        stat = jnp.where(mine, near[:, half:], far[:, half:]).astype(jnp.float32)
        r_lse = res_lse[side]
        for h in range(heads):
            pre = (
                stat[:, h : h + 1] + stat[:, heads + h : heads + h + 1] + stat[:, 2 * heads + h : 2 * heads + h + 1]
            )
            weight = 1.0 / (1.0 + jnp.exp(r_lse[:, h : h + 1] - pre))
            cols = slice(h * HD, (h + 1) * HD)
            r = res[side, :, cols]
            x = jnp.where(mine, near[:, cols].astype(jnp.float32), far[:, cols].astype(jnp.float32))
            y = jnp.where(is_reader > 0, r + weight * (x - r), r)
            attn[:, side * half + h * HD : side * half + (h + 1) * HD] = y.astype(jnp.bfloat16)
    project(attn[...], w, outs, 0, width)
    for copy in copies:
        copy.wait()


def home_kernel(width, attn, *refs):
    project(attn[...], refs[:-1], refs[-1:], 0, width)


def shards(n_dp, n_tp, queries, prefix_kv, cache_kv, lengths, page_table, owner, readers, w_out):
    rows = queries.shape[0]
    heads = queries.shape[1] // HD
    groups = prefix_kv.shape[2] // HD
    group = heads // groups
    prefix = prefix_kv.shape[1]
    maxpages = page_table.shape[1] // rows
    n_readers = readers.shape[0]
    chips = n_dp // 2
    half_groups = max(groups // 2, 1)
    half_heads = heads // 2
    share_group = half_heads // half_groups
    half = half_heads * HD
    wide = half + 128
    d_out = w_out.shape[1]
    chunk = d_out // n_tp

    def hop(x, d):
        return lax.ppermute(x, "dp", [(i, i ^ d) for i in range(n_dp)])

    mine, other = pl.pallas_call(
        functools.partial(split_kernel, half),
        out_shape=tuple(jax.ShapeDtypeStruct((rows, half), jnp.bfloat16) for _ in range(2)),
        in_specs=[vmem_spec()],
        out_specs=(vmem_spec(), vmem_spec()),
        compiler_params=pltpu.CompilerParams(vmem_limit_bytes=2 << 20),
        name="split",
    )(queries)
    got = hop(other, 1)
    kv_cols = half_groups * HD
    shared = pl.pallas_call(
        functools.partial(share_kernel, kv_cols),
        out_shape=jax.ShapeDtypeStruct((2, prefix, kv_cols), jnp.bfloat16),
        in_specs=[hbm_spec(), vmem_spec()],
        out_specs=vmem_spec(),
        scratch_shapes=[pltpu.SemaphoreType.DMA(())],
        compiler_params=pltpu.CompilerParams(vmem_limit_bytes=4 << 20),
        cost_estimate=pl.CostEstimate(flops=1 << 24, bytes_accessed=4 * prefix * kv_cols, transcendentals=0),
        name="share",
    )(in_hbm(prefix_kv), other)
    pair = pl.pallas_call(
        pair_kernel,
        out_shape=jax.ShapeDtypeStruct((2, rows, half), jnp.bfloat16),
        in_specs=[vmem_spec()] * 3,
        out_specs=vmem_spec(),
        compiler_params=pltpu.CompilerParams(vmem_limit_bytes=2 << 20),
        cost_estimate=pl.CostEstimate(flops=1 << 32, bytes_accessed=1 << 24, transcendentals=0),
        name="pair",
    )(mine, got, shared)
    mate_kv = hop(shared, 1)
    gathered = [pair] + [hop(pair, 2 * d) for d in range(1, chips)]

    m_rows = group * rows
    width = min(512, chunk)
    plan = (n_tp, chunk, width)
    last = min(2, chunk // width)
    counts = (1, d_out // width - 1 - last, last)

    def w_outs(n):
        return tuple(VMEM((w_out.shape[0], width), w_out.dtype) for _ in range(n))

    res, res_lse, own_kv, *w_parts = pl.pallas_call(
        functools.partial(resident_kernel, rows, groups, group, maxpages, plan, counts[0]),
        out_shape=(
            jax.ShapeDtypeStruct((2, rows, half), jnp.float32),
            jax.ShapeDtypeStruct((2, rows, 128), jnp.float32),
            jax.ShapeDtypeStruct((2, prefix, kv_cols), jnp.bfloat16),
        )
        + w_outs(counts[0]),
        in_specs=[smem_spec(), smem_spec(), vmem_spec(), hbm_spec(), hbm_spec(), hbm_spec()],
        out_specs=(vmem_spec(),) * (3 + counts[0]),
        scratch_shapes=[
            VMEM((rows, maxpages, PAGE, groups * HD), jnp.bfloat16),
            VMEM((rows, maxpages, PAGE, groups * HD), jnp.bfloat16),
            pltpu.SemaphoreType.DMA((2, rows)),
            pltpu.SemaphoreType.DMA(()),
            pltpu.SemaphoreType.DMA((counts[0],)),
        ],
        compiler_params=pltpu.CompilerParams(vmem_limit_bytes=13 << 20),
        cost_estimate=pl.CostEstimate(
            flops=4 * heads * rows * rows * maxpages * PAGE * HD,
            bytes_accessed=2 * rows * maxpages * PAGE * groups * HD * 2,
            transcendentals=groups * m_rows * maxpages * PAGE,
        ),
        name="resident",
    )(page_table[0], lengths, queries, in_hbm(cache_kv), in_hbm(prefix_kv), in_hbm(w_out))

    total = share_group * n_readers * rows
    block = min(256, total)
    pre = pl.pallas_call(
        functools.partial(
            prefix_kernel, chips, rows, half_groups, share_group, n_readers, block, plan, counts[0], counts[1]
        ),
        out_shape=tuple(jax.ShapeDtypeStruct((2, rows, wide), jnp.bfloat16) for _ in range(chips))
        + w_outs(counts[1]),
        in_specs=[smem_spec(), smem_spec()] + [vmem_spec()] * (chips + 2) + [hbm_spec()],
        out_specs=(vmem_spec(),) * (chips + counts[1]),
        scratch_shapes=[
            VMEM((2 * chips, rows, half), jnp.float32),
            VMEM((half_groups, total, HD), jnp.float32),
            VMEM((half_groups, total, HD), jnp.float32),
            VMEM((half_groups, total, 128), jnp.float32),
            VMEM((2 * chips, rows, wide), jnp.float32),
            pltpu.SemaphoreType.DMA((counts[1],)),
        ],
        compiler_params=pltpu.CompilerParams(vmem_limit_bytes=12 << 20),
        cost_estimate=pl.CostEstimate(
            flops=4 * half_groups * total * prefix * HD,
            bytes_accessed=4 * half_groups * prefix * HD,
            transcendentals=half_groups * total * prefix,
        ),
        name="prefix",
    )(owner, readers, *gathered, own_kv, mate_kv, in_hbm(w_out))
    w_parts = [pltpu.with_memory_space_constraint(x, VMEM) for x in list(w_parts) + list(pre[chips:])]

    back = [pre[0]] + [hop(pre[d], 2 * d) for d in range(1, chips)]
    near, other = pl.pallas_call(
        functools.partial(choose_kernel, chips),
        out_shape=tuple(jax.ShapeDtypeStruct((rows, wide), jnp.bfloat16) for _ in range(2)),
        in_specs=[smem_spec()] + [vmem_spec()] * chips,
        out_specs=(vmem_spec(), vmem_spec()),
        compiler_params=pltpu.CompilerParams(vmem_limit_bytes=4 << 20),
        name="choose",
    )(owner, *back)
    far = hop(other, 1)


    per_chunk = chunk // width
    cost = pl.CostEstimate(
        flops=2 * rows * heads * HD * chunk * 16, bytes_accessed=2 * heads * HD * chunk, transcendentals=0
    )
    projected = pl.pallas_call(
        functools.partial(away_kernel, half_heads, plan, len(w_parts), counts[2]),
        out_shape=tuple(jax.ShapeDtypeStruct((rows, chunk), jnp.float32) for _ in range(n_tp - 1))
        + (jax.ShapeDtypeStruct((rows, heads * HD), jnp.bfloat16),)
        + w_outs(counts[2]),
        in_specs=[smem_spec()] + [vmem_spec()] * 4 + [hbm_spec()] + [vmem_spec()] * len(w_parts),
        out_specs=(vmem_spec(),) * (n_tp + counts[2]),
        scratch_shapes=[pltpu.SemaphoreType.DMA((counts[2],))],
        compiler_params=pltpu.CompilerParams(vmem_limit_bytes=4 << 20),
        cost_estimate=cost,
        name="away",
    )(readers, near, far, res, res_lse, in_hbm(w_out), *w_parts)
    away, attn = projected[: n_tp - 1], projected[n_tp - 1]
    w_parts = (w_parts + list(projected[n_tp:]))[-per_chunk:]
    home = pl.pallas_call(
        functools.partial(home_kernel, width),
        out_shape=jax.ShapeDtypeStruct((rows, chunk), jnp.float32),
        in_specs=[vmem_spec()] * (1 + per_chunk),
        out_specs=vmem_spec(),
        compiler_params=pltpu.CompilerParams(vmem_limit_bytes=4 << 20),
        cost_estimate=cost,
        name="home",
    )(attn, *w_parts)
    for k in range(1, n_tp):
        home = home + lax.ppermute(away[k - 1], "tp", [(i, i ^ k) for i in range(n_tp)])
    return home.astype(jnp.bfloat16)


def solution(mesh):
    placed = (
        P("dp", "tp"),
        P(None, "dp", "tp"),
        P(None, "dp", None, "tp"),
        P("dp"),
        P("dp", None),
        P(),
        P(),
        P("tp", None),
    )
    return jax.shard_map(
        functools.partial(shards, mesh.shape["dp"], mesh.shape["tp"]),
        mesh=mesh,
        in_specs=placed,
        out_specs=P("dp", "tp"),
        check_vma=False,
    )
```

time: 171 us -> 68.3 us (0.40)
  waiting for transfers between devices: 83.2 us -> 11.8 us
  local copies, waits for them, and re-layouts: 47.4 us -> 0.86 us
  starting transfers between devices: 0.04 us -> 30.1 us
  Pallas kernels: 0 us -> 24.7 us
  matrix products: 19.8 us -> 0 us
  between operations: 13.5 us -> 0.14 us
  other arithmetic: 5.81 us -> 0.62 us
    psum x1 -> x0, waiting for transfers between devices: 73.5 us -> none  [from_root(): return lax.psum(block, axis)]
    ppermute x0 -> x18, starting transfers between devices: none -> 30.1 us  [the longest x17 28.5 us: hop(): return lax.ppermute(x, 'dp', [(i, i ^ d) for i in range(n_dp)])]
    pallas_call x0 -> x8, Pallas kernels: none -> 24.7 us  [the longest x1 7.73 us: shards(): pl.pallas_call(functools.partial(prefix_kernel, chips, rows, half_groups,...]
    dot_general x5 -> x0, matrix products: 19.8 us -> none  [the longest x1 13.5 us: shards(): partial_out = jnp.dot(attn, w_out, preferred_element_type=jnp.float32)]
    gather x2 -> x0, local copies, waits for them, and re-layouts: 16.8 us -> none  [shards(): cache_kv[:, pages].reshape(2, rows, maxpages * PAGE, groups_here, HD)]
    squeeze x2 -> x0, local copies, waits for them, and re-layouts: 14 us -> none  [the longest x1 6.99 us: shards(): resident[1]]
    ppermute x0 -> x18, waiting for transfers between devices: none -> 11.8 us  [the longest x17 11.3 us: hop(): return lax.ppermute(x, 'dp', [(i, i ^ d) for i in range(n_dp)])]
    reduce_scatter x1 -> x0, waiting for transfers between devices: 9.65 us -> none  [shards(): lax.psum_scatter(partial_out, 'tp', scatter_dimension=1, tiled=True)]
  transfers between devices with their start and end apart: 2 -> 18, of which waited for: 2 -> 8; matrix products, arithmetic and copies ran while one was open for 25% -> 0% of each run, Pallas kernels for 0% -> 12%
where the time goes in v1:
time: 68.3 us; the launch traced here: 68.2 us
  starting transfers between devices  30.1 us (44%)
  Pallas kernels  24.7 us (36%)
  waiting for transfers between devices  11.8 us (17%)
  local copies, waits for them, and re-layouts  0.86 us (1%)
    ppermute x17, starting transfers between devices, hop(): return lax.ppermute(x, 'dp', [(i, i ^ d) for i in range(n_dp)])  28.5 us
    ppermute x17, waiting for transfers between devices, hop(): return lax.ppermute(x, 'dp', [(i, i ^ d) for i in range(n_dp)])  11.3 us
    pallas_call x1, Pallas kernels, shards(): pl.pallas_call(functools.partial(prefix_kernel, chips, rows, half_groups,...  7.73 us
    pallas_call x1, Pallas kernels, shards(): pl.pallas_call(functools.partial(away_kernel, half_heads, plan, len(w_par...  6.32 us
    pallas_call x1, Pallas kernels, shards(): pl.pallas_call(functools.partial(resident_kernel, rows, groups, group, ma...  6.16 us
    pallas_call x1, Pallas kernels, shards(): pl.pallas_call(functools.partial(home_kernel, width), out_shape=jax.Shape...  2.26 us
    pallas_call x1, Pallas kernels, shards(): pl.pallas_call(functools.partial(share_kernel, kv_cols), out_shape=jax.Sh...  1.6 us
    ppermute x1, starting transfers between devices, shards(): lax.ppermute(away[k - 1], 'tp', [(i, i ^ k) for i in range(n_tp)])  1.58 us
  transfers between devices with their start and end apart: 18, of which 8 were waited for; matrix products, arithmetic and copies ran while one was open for 0% of the time, Pallas kernels for 12%

profile of v1, /device:TPU:0, one launch (start us, length us, event | category | flops | bytes accessed | tf_op | source)
XLA Modules:
  0.0 68.2 jit_solution(13058156119131937670)
XLA Ops:
  0.0 0.8 %copy-done = bf16[8,4096]{1,0:T(8,128)(2,1)S(1)} copy-done((bf16[8,4096]{1,0:T(8,128)(2,1)S(1)}, bf16[8,4096]{1,0:T(8,128)(2,1)}, u32[]{:S(2)}) %copy-start) | copy-done | bytes 65560
  0.8 1.6 %share.1.after = bf16[2,2048,256]{2,1,0:T(8,128)(2,1)S(1)} custom-call(bf16[2,2048,512]{2,1,0:T(8,128)(2,1)} %kv.3, bf16[8,2048]{1,0:T(8,128)(2,1)S(1)} %get-tuple-element.31.after), custom_call_target="tpu_custom_call" | custom-call | flops 16777216 | bytes 2097152 | tf_op jit(solution)/shard_map/share/pallas_call | solution.py:303
  3.1 3.8 %collective-permute-done.got = bf16[8,2048]{1,0:T(8,128)(2,1)S(1)} collective-permute-done((bf16[8,2048]{1,0:T(8,128)(2,1)S(1)}, bf16[8,2048]{1,0:T(8,128)(2,1)S(1)}, u32[]{:S(2)}, u32[]{:S(2)}) %collective-permute-start) | collective-permute-done | bytes 32800 | tf_op jit(solution)/shard_map/ppermute | solution.py:291
  6.9 6.0 %collective-permute-start.7 = (bf16[2,8,2048]{2,1,0:T(8,128)(2,1)S(1)}, bf16[2,8,2048]{2,1,0:T(8,128)(2,1)S(1)}, u32[]{:S(2)}, u32[]{:S(2)}) collective-permute-start(bf16[2,8,2048]{2,1,0:T(8,128)(2,1)S(1)} %pair.1.refs_0_), channel_id=1, source_target_pairs={{0,28},{2,30},{4,24},{6,26},{8,20},{10,22},{12,16},{14,18},{16,12}... | collective-permute-start | bytes 196616 | tf_op jit(solution)/shard_map/ppermute | solution.py:291
  13.0 0.8 %collective-permute-start.5 = (bf16[2,8,2048]{2,1,0:T(8,128)(2,1)S(1)}, bf16[2,8,2048]{2,1,0:T(8,128)(2,1)S(1)}, u32[]{:S(2)}, u32[]{:S(2)}) collective-permute-start(bf16[2,8,2048]{2,1,0:T(8,128)(2,1)S(1)} %pair.1.refs_0_), channel_id=1, source_target_pairs={{0,20},{2,22},{4,16},{6,18},{8,28},{10,30},{12,24},{14,26},{16,4},... | collective-permute-start | bytes 196616 | tf_op jit(solution)/shard_map/ppermute | solution.py:291
  13.8 2.0 %collective-permute-start.4 = (bf16[2,8,2048]{2,1,0:T(8,128)(2,1)S(1)}, bf16[2,8,2048]{2,1,0:T(8,128)(2,1)S(1)}, u32[]{:S(2)}, u32[]{:S(2)}) collective-permute-start(bf16[2,8,2048]{2,1,0:T(8,128)(2,1)S(1)} %pair.1.refs_0_), channel_id=1, source_target_pairs={{0,16},{2,18},{4,20},{6,22},{8,24},{10,26},{12,28},{14,30},{16,0},... | collective-permute-start | bytes 196616 | tf_op jit(solution)/shard_map/ppermute | solution.py:291
  15.8 2.3 %collective-permute-start.3 = (bf16[2,8,2048]{2,1,0:T(8,128)(2,1)S(1)}, bf16[2,8,2048]{2,1,0:T(8,128)(2,1)S(1)}, u32[]{:S(2)}, u32[]{:S(2)}) collective-permute-start(bf16[2,8,2048]{2,1,0:T(8,128)(2,1)S(1)} %pair.1.refs_0_), channel_id=1, source_target_pairs={{0,12},{2,14},{4,8},{6,10},{8,4},{10,6},{12,0},{14,2},{16,28},{18,... | collective-permute-start | bytes 196616 | tf_op jit(solution)/shard_map/ppermute | solution.py:291
  18.1 1.3 %collective-permute-done.6.refs_6_ = bf16[2,8,2048]{2,1,0:T(8,128)(2,1)S(1)} collective-permute-done((bf16[2,8,2048]{2,1,0:T(8,128)(2,1)S(1)}, bf16[2,8,2048]{2,1,0:T(8,128)(2,1)S(1)}, u32[]{:S(2)}, u32[]{:S(2)}) %collective-permute-start.6) | collective-permute-done | bytes 65568 | tf_op jit(solution)/shard_map/ppermute | solution.py:291
  19.4 3.2 %collective-permute-start.2 = (bf16[2,8,2048]{2,1,0:T(8,128)(2,1)S(1)}, bf16[2,8,2048]{2,1,0:T(8,128)(2,1)S(1)}, u32[]{:S(2)}, u32[]{:S(2)}) collective-permute-start(bf16[2,8,2048]{2,1,0:T(8,128)(2,1)S(1)} %pair.1.refs_0_), channel_id=1, source_target_pairs={{0,8},{2,10},{4,12},{6,14},{8,0},{10,2},{12,4},{14,6},{16,24},{18,... | collective-permute-start | bytes 196616 | tf_op jit(solution)/shard_map/ppermute | solution.py:291
  22.8 2.2 %collective-permute-start.1 = (bf16[2,8,2048]{2,1,0:T(8,128)(2,1)S(1)}, bf16[2,8,2048]{2,1,0:T(8,128)(2,1)S(1)}, u32[]{:S(2)}, u32[]{:S(2)}) collective-permute-start(bf16[2,8,2048]{2,1,0:T(8,128)(2,1)S(1)} %pair.1.refs_0_), channel_id=1, source_target_pairs={{0,4},{2,6},{4,0},{6,2},{8,12},{10,14},{12,8},{14,10},{16,20},{18,... | collective-permute-start | bytes 196616 | tf_op jit(solution)/shard_map/ppermute | solution.py:291
  25.0 6.2 %resident.1 = (f32[2,8,2048]{2,1,0:T(8,128)S(1)}, f32[2,8,128]{2,1,0:T(8,128)S(1)}, bf16[2,2048,256]{2,1,0:T(8,128)(2,1)S(1)}, bf16[4096,512]{1,0:T(8,128)(2,1)S(1)}) custom-call(s32[64]{0:T(128)S(1)} %bitcast.1, s32[8]{0:T(128)S(1)} %copy-done.5, bf16[8,4096]{1,0:T(8,128)(2,1)S(1)} %copy-done.1, bf16[2,64,64,512]{3,2,1,0:T(8,128)(2,1)} %cache.1, ...), custom_call_target="tpu_custom_call" | custom-call | flops 536870912 | bytes 8388608 | tf_op jit(solution)/shard_map/resident/pallas_call | solution.py:334
  31.3 7.7 %prefix.1 = (bf16[2,8,2176]{2,1,0:T(8,128)(2,1)S(1)}, bf16[2,8,2176]{2,1,0:T(8,128)(2,1)S(1)}, bf16[2,8,2176]{2,1,0:T(8,128)(2,1)S(1)}, bf16[2,8,2176]{2,1,0:T(8...) custom-call(s32[16]{0:T(128)S(1)} %copy-done.2, ...), custom_call_target="tpu_custom_call" | custom-call | flops 1073741824 | bytes 2097152 | tf_op jit(solution)/shard_map/prefix/pallas_call | solution.py:362
  39.2 3.3 %collective-permute-start.11 = (bf16[2,8,2176]{2,1,0:T(8,128)(2,1)S(1)}, bf16[2,8,2176]{2,1,0:T(8,128)(2,1)S(1)}, u32[]{:S(2)}, u32[]{:S(2)}) collective-permute-start(bf16[2,8,2176]{2,1,0:T(8,128)(2,1)S(1)} %get-tuple-element.36), channel_id=1, source_target_pairs={{0,12},{2,14},{4,8},{6,10},{8,4},{10,6},{12,0},{14,2},{16,28},{18,... | collective-permute-start | bytes 208904 | tf_op jit(solution)/shard_map/ppermute | solution.py:291
  42.5 1.1 %collective-permute-start.12 = (bf16[2,8,2176]{2,1,0:T(8,128)(2,1)S(1)}, bf16[2,8,2176]{2,1,0:T(8,128)(2,1)S(1)}, u32[]{:S(2)}, u32[]{:S(2)}) collective-permute-start(bf16[2,8,2176]{2,1,0:T(8,128)(2,1)S(1)} %get-tuple-element.37), channel_id=1, source_target_pairs={{0,16},{2,18},{4,20},{6,22},{8,24},{10,26},{12,28},{14,30},{16,0},... | collective-permute-start | bytes 208904 | tf_op jit(solution)/shard_map/ppermute | solution.py:291
  43.6 1.4 %collective-permute-start.13 = (bf16[2,8,2176]{2,1,0:T(8,128)(2,1)S(1)}, bf16[2,8,2176]{2,1,0:T(8,128)(2,1)S(1)}, u32[]{:S(2)}, u32[]{:S(2)}) collective-permute-start(bf16[2,8,2176]{2,1,0:T(8,128)(2,1)S(1)} %get-tuple-element.38), channel_id=1, source_target_pairs={{0,20},{2,22},{4,16},{6,18},{8,28},{10,30},{12,24},{14,26},{16,4},... | collective-permute-start | bytes 208904 | tf_op jit(solution)/shard_map/ppermute | solution.py:291
  45.0 2.9 %collective-permute-start.14 = (bf16[2,8,2176]{2,1,0:T(8,128)(2,1)S(1)}, bf16[2,8,2176]{2,1,0:T(8,128)(2,1)S(1)}, u32[]{:S(2)}, u32[]{:S(2)}) collective-permute-start(bf16[2,8,2176]{2,1,0:T(8,128)(2,1)S(1)} %get-tuple-element.39), channel_id=1, source_target_pairs={{0,24},{2,26},{4,28},{6,30},{8,16},{10,18},{12,20},{14,22},{16,8},... | collective-permute-start | bytes 208904 | tf_op jit(solution)/shard_map/ppermute | solution.py:291
  47.9 2.3 %collective-permute-start.15 = (bf16[2,8,2176]{2,1,0:T(8,128)(2,1)S(1)}, bf16[2,8,2176]{2,1,0:T(8,128)(2,1)S(1)}, u32[]{:S(2)}, u32[]{:S(2)}) collective-permute-start(bf16[2,8,2176]{2,1,0:T(8,128)(2,1)S(1)} %get-tuple-element.40), channel_id=1, source_target_pairs={{0,28},{2,30},{4,24},{6,26},{8,20},{10,22},{12,16},{14,18},{16,12}... | collective-permute-start | bytes 208904 | tf_op jit(solution)/shard_map/ppermute | solution.py:291
  50.2 1.9 %collective-permute-done.12.refs_4_ = bf16[2,8,2176]{2,1,0:T(8,128)(2,1)S(1)} collective-permute-done((bf16[2,8,2176]{2,1,0:T(8,128)(2,1)S(1)}, bf16[2,8,2176]{2,1,0:T(8,128)(2,1)S(1)}, u32[]{:S(2)}, u32[]{:S(2)}) %collective-permute-start.12) | collective-permute-done | bytes 69664 | tf_op jit(solution)/shard_map/ppermute | solution.py:291
  52.1 1.2 %collective-permute-done.13.refs_5_ = bf16[2,8,2176]{2,1,0:T(8,128)(2,1)S(1)} collective-permute-done((bf16[2,8,2176]{2,1,0:T(8,128)(2,1)S(1)}, bf16[2,8,2176]{2,1,0:T(8,128)(2,1)S(1)}, u32[]{:S(2)}, u32[]{:S(2)}) %collective-permute-start.13) | collective-permute-done | bytes 69664 | tf_op jit(solution)/shard_map/ppermute | solution.py:291
  53.3 1.7 %collective-permute-done.15.refs_7_ = bf16[2,8,2176]{2,1,0:T(8,128)(2,1)S(1)} collective-permute-done((bf16[2,8,2176]{2,1,0:T(8,128)(2,1)S(1)}, bf16[2,8,2176]{2,1,0:T(8,128)(2,1)S(1)}, u32[]{:S(2)}, u32[]{:S(2)}) %collective-permute-start.15) | collective-permute-done | bytes 69664 | tf_op jit(solution)/shard_map/ppermute | solution.py:291
  55.7 1.2 %collective-permute-done.16.far = bf16[8,2176]{1,0:T(8,128)(2,1)S(1)} collective-permute-done((bf16[8,2176]{1,0:T(8,128)(2,1)S(1)}, bf16[8,2176]{1,0:T(8,128)(2,1)S(1)}, u32[]{:S(2)}, u32[]{:S(2)}) %collective-permute-start.16) | collective-permute-done | bytes 34848 | tf_op jit(solution)/shard_map/ppermute | solution.py:291
  56.9 6.3 %away.1 = (f32[8,2048]{1,0:T(8,128)S(1)}, bf16[8,4096]{1,0:T(8,128)(2,1)S(1)}, bf16[4096,512]{1,0:T(8,128)(2,1)S(1)}, bf16[4096,512]{1,0:T(8,128)(2,1)S(1)}) custom-call(s32[8]{0:T(128)S(1)} %copy-done.3, bf16[8,2176]{1,0:T(8,128)(2,1)S(1)} %get-tuple-element.41.near, bf16[8,2176]{1,0:T(8,128)(2,1)S(1)} %collective-permute-done.16.far, ...), custom_call_target="tpu_custom_call" | custom-call | flops 2147483648 | bytes 16777216 | tf_op jit(solution)/shard_map/away/pallas_call | solution.py:404
  63.2 1.6 %collective-permute-start.17 = (f32[8,2048]{1,0:T(8,128)S(1)}, f32[8,2048]{1,0:T(8,128)S(1)}, u32[]{:S(2)}, u32[]{:S(2)}) collective-permute-start(f32[8,2048]{1,0:T(8,128)S(1)} %get-tuple-element.54), channel_id=1, source_target_pairs={{0,1},{1,0},{2,3},{3,2},{4,5},{5,4},{6,7},{7,6},{8,9},{9,8},{10,11... | collective-permute-start | bytes 196616 | tf_op jit(solution)/shard_map/ppermute | solution.py:428
  64.8 2.3 %home.1 = f32[8,2048]{1,0:T(8,128)S(1)} custom-call(bf16[8,4096]{1,0:T(8,128)(2,1)S(1)} %get-tuple-element.51.attn, bf16[4096,512]{1,0:T(8,128)(2,1)S(1)} %get-tuple-element.49.refs_4_.refs_0_, bf16[4096,512]{1,0:T(8,128)(2,1)S(1)} %get-tuple-element.50.refs_5_.refs_1_, bf16[4096,512]{1,0:T(8,128)(2,1)S(1)} %get-tuple-element.52.refs_2_, ...), custom_call_target="tpu_custom_call" | custom-call | flops 2147483648 | bytes 16777216 | tf_op jit(solution)/shard_map/home/pallas_call | solution.py:418
  (33 shorter events, 3.2 us)
Async XLA Ops:
  0.0 0.8 %copy-start = (bf16[8,4096]{1,0:T(8,128)(2,1)S(1)}, bf16[8,4096]{1,0:T(8,128)(2,1)}, u32[]{:S(2)}) copy-start(bf16[8,4096]{1,0:T(8,128)(2,1)} %q_ref.3) | copy-start | bytes 196612
  2.5 28.8 %collective-permute-start.8 = (bf16[2,2048,256]{2,1,0:T(8,128)(2,1)S(1)}, bf16[2,2048,256]{2,1,0:T(8,128)(2,1)S(1)}, u32[]{:S(2)}, u32[]{:S(2)}) collective-permute-start(bf16[2,2048,256]{2,1,0:T(8,128)(2,1)S(1)} %share.1.after), channel_id=1, source_target_pairs={{0,2},{2,0},{4,6},{6,4},{8,10},{10,8},{12,14},{14,12},{16,18},{18,... | collective-permute-start | bytes 6291464 | tf_op jit(solution)/shard_map/ppermute | solution.py:291
  3.0 3.8 %collective-permute-start = (bf16[8,2048]{1,0:T(8,128)(2,1)S(1)}, bf16[8,2048]{1,0:T(8,128)(2,1)S(1)}, u32[]{:S(2)}, u32[]{:S(2)}) collective-permute-start(bf16[8,2048]{1,0:T(8,128)(2,1)S(1)} %get-tuple-element.31.after), channel_id=1, source_target_pairs={{0,2},{2,0},{4,6},{6,4},{8,10},{10,8},{12,14},{14,12},{16,18},{18,... | collective-permute-start | bytes 98312 | tf_op jit(solution)/shard_map/ppermute | solution.py:291
  6.8 18.1 %copy-start.1 = (bf16[8,4096]{1,0:T(8,128)(2,1)S(1)}, bf16[8,4096]{1,0:T(8,128)(2,1)}, u32[]{:S(2)}) copy-start(bf16[8,4096]{1,0:T(8,128)(2,1)} %q_ref.3) | copy-start | bytes 196612
  6.8 18.1 %copy-start.4 = (s32[1,64]{1,0:T(1,128)S(1)}, s32[1,64]{1,0:T(1,128)}, u32[]{:S(2)}) copy-start(s32[1,64]{1,0:T(1,128)} %param.12) | copy-start | bytes 772
  6.8 18.1 %copy-start.5 = (s32[8]{0:T(128)S(1)}, s32[8]{0:T(128)}, u32[]{:S(2)}) copy-start(s32[8]{0:T(128)} %lengths.1) | copy-start | bytes 100
  6.9 9.0 %collective-permute-start.7 = (bf16[2,8,2048]{2,1,0:T(8,128)(2,1)S(1)}, bf16[2,8,2048]{2,1,0:T(8,128)(2,1)S(1)}, u32[]{:S(2)}, u32[]{:S(2)}) collective-permute-start(bf16[2,8,2048]{2,1,0:T(8,128)(2,1)S(1)} %pair.1.refs_0_), channel_id=1, source_target_pairs={{0,28},{2,30},{4,24},{6,26},{8,20},{10,22},{12,16},{14,18},{16,12}... | collective-permute-start | bytes 196616 | tf_op jit(solution)/shard_map/ppermute | solution.py:291
  12.8 6.6 %collective-permute-start.6 = (bf16[2,8,2048]{2,1,0:T(8,128)(2,1)S(1)}, bf16[2,8,2048]{2,1,0:T(8,128)(2,1)S(1)}, u32[]{:S(2)}, u32[]{:S(2)}) collective-permute-start(bf16[2,8,2048]{2,1,0:T(8,128)(2,1)S(1)} %pair.1.refs_0_), channel_id=1, source_target_pairs={{0,24},{2,26},{4,28},{6,30},{8,16},{10,18},{12,20},{14,22},{16,8},... | collective-permute-start | bytes 196616 | tf_op jit(solution)/shard_map/ppermute | solution.py:291
  13.0 9.8 %collective-permute-start.5 = (bf16[2,8,2048]{2,1,0:T(8,128)(2,1)S(1)}, bf16[2,8,2048]{2,1,0:T(8,128)(2,1)S(1)}, u32[]{:S(2)}, u32[]{:S(2)}) collective-permute-start(bf16[2,8,2048]{2,1,0:T(8,128)(2,1)S(1)} %pair.1.refs_0_), channel_id=1, source_target_pairs={{0,20},{2,22},{4,16},{6,18},{8,28},{10,30},{12,24},{14,26},{16,4},... | collective-permute-start | bytes 196616 | tf_op jit(solution)/shard_map/ppermute | solution.py:291
  13.8 17.4 %collective-permute-start.4 = (bf16[2,8,2048]{2,1,0:T(8,128)(2,1)S(1)}, bf16[2,8,2048]{2,1,0:T(8,128)(2,1)S(1)}, u32[]{:S(2)}, u32[]{:S(2)}) collective-permute-start(bf16[2,8,2048]{2,1,0:T(8,128)(2,1)S(1)} %pair.1.refs_0_), channel_id=1, source_target_pairs={{0,16},{2,18},{4,20},{6,22},{8,24},{10,26},{12,28},{14,30},{16,0},... | collective-permute-start | bytes 196616 | tf_op jit(solution)/shard_map/ppermute | solution.py:291
  15.8 15.4 %collective-permute-start.3 = (bf16[2,8,2048]{2,1,0:T(8,128)(2,1)S(1)}, bf16[2,8,2048]{2,1,0:T(8,128)(2,1)S(1)}, u32[]{:S(2)}, u32[]{:S(2)}) collective-permute-start(bf16[2,8,2048]{2,1,0:T(8,128)(2,1)S(1)} %pair.1.refs_0_), channel_id=1, source_target_pairs={{0,12},{2,14},{4,8},{6,10},{8,4},{10,6},{12,0},{14,2},{16,28},{18,... | collective-permute-start | bytes 196616 | tf_op jit(solution)/shard_map/ppermute | solution.py:291
  19.4 11.8 %collective-permute-start.2 = (bf16[2,8,2048]{2,1,0:T(8,128)(2,1)S(1)}, bf16[2,8,2048]{2,1,0:T(8,128)(2,1)S(1)}, u32[]{:S(2)}, u32[]{:S(2)}) collective-permute-start(bf16[2,8,2048]{2,1,0:T(8,128)(2,1)S(1)} %pair.1.refs_0_), channel_id=1, source_target_pairs={{0,8},{2,10},{4,12},{6,14},{8,0},{10,2},{12,4},{14,6},{16,24},{18,... | collective-permute-start | bytes 196616 | tf_op jit(solution)/shard_map/ppermute | solution.py:291
  22.8 8.4 %collective-permute-start.1 = (bf16[2,8,2048]{2,1,0:T(8,128)(2,1)S(1)}, bf16[2,8,2048]{2,1,0:T(8,128)(2,1)S(1)}, u32[]{:S(2)}, u32[]{:S(2)}) collective-permute-start(bf16[2,8,2048]{2,1,0:T(8,128)(2,1)S(1)} %pair.1.refs_0_), channel_id=1, source_target_pairs={{0,4},{2,6},{4,0},{6,2},{8,12},{10,14},{12,8},{14,10},{16,20},{18,... | collective-permute-start | bytes 196616 | tf_op jit(solution)/shard_map/ppermute | solution.py:291
  25.0 6.2 %copy-start.2 = (s32[16]{0:T(128)S(1)}, s32[16]{0:T(128)}, u32[]{:S(2)}) copy-start(s32[16]{0:T(128)} %owner.1) | copy-start | bytes 196
  25.0 6.2 %copy-start.3 = (s32[8]{0:T(128)S(1)}, s32[8]{0:T(128)}, u32[]{:S(2)}) copy-start(s32[8]{0:T(128)} %readers.3) | copy-start | bytes 100
  39.0 6.0 %collective-permute-start.9 = (bf16[2,8,2176]{2,1,0:T(8,128)(2,1)S(1)}, bf16[2,8,2176]{2,1,0:T(8,128)(2,1)S(1)}, u32[]{:S(2)}, u32[]{:S(2)}) collective-permute-start(bf16[2,8,2176]{2,1,0:T(8,128)(2,1)S(1)} %get-tuple-element.34), channel_id=1, source_target_pairs={{0,4},{2,6},{4,0},{6,2},{8,12},{10,14},{12,8},{14,10},{16,20},{18,... | collective-permute-start | bytes 208904 | tf_op jit(solution)/shard_map/ppermute | solution.py:291
  39.1 8.8 %collective-permute-start.10 = (bf16[2,8,2176]{2,1,0:T(8,128)(2,1)S(1)}, bf16[2,8,2176]{2,1,0:T(8,128)(2,1)S(1)}, u32[]{:S(2)}, u32[]{:S(2)}) collective-permute-start(bf16[2,8,2176]{2,1,0:T(8,128)(2,1)S(1)} %get-tuple-element.35), channel_id=1, source_target_pairs={{0,8},{2,10},{4,12},{6,14},{8,0},{10,2},{12,4},{14,6},{16,24},{18,... | collective-permute-start | bytes 208904 | tf_op jit(solution)/shard_map/ppermute | solution.py:291
  39.2 11.0 %collective-permute-start.11 = (bf16[2,8,2176]{2,1,0:T(8,128)(2,1)S(1)}, bf16[2,8,2176]{2,1,0:T(8,128)(2,1)S(1)}, u32[]{:S(2)}, u32[]{:S(2)}) collective-permute-start(bf16[2,8,2176]{2,1,0:T(8,128)(2,1)S(1)} %get-tuple-element.36), channel_id=1, source_target_pairs={{0,12},{2,14},{4,8},{6,10},{8,4},{10,6},{12,0},{14,2},{16,28},{18,... | collective-permute-start | bytes 208904 | tf_op jit(solution)/shard_map/ppermute | solution.py:291
  42.5 9.5 %collective-permute-start.12 = (bf16[2,8,2176]{2,1,0:T(8,128)(2,1)S(1)}, bf16[2,8,2176]{2,1,0:T(8,128)(2,1)S(1)}, u32[]{:S(2)}, u32[]{:S(2)}) collective-permute-start(bf16[2,8,2176]{2,1,0:T(8,128)(2,1)S(1)} %get-tuple-element.37), channel_id=1, source_target_pairs={{0,16},{2,18},{4,20},{6,22},{8,24},{10,26},{12,28},{14,30},{16,0},... | collective-permute-start | bytes 208904 | tf_op jit(solution)/shard_map/ppermute | solution.py:291
  43.6 9.7 %collective-permute-start.13 = (bf16[2,8,2176]{2,1,0:T(8,128)(2,1)S(1)}, bf16[2,8,2176]{2,1,0:T(8,128)(2,1)S(1)}, u32[]{:S(2)}, u32[]{:S(2)}) collective-permute-start(bf16[2,8,2176]{2,1,0:T(8,128)(2,1)S(1)} %get-tuple-element.38), channel_id=1, source_target_pairs={{0,20},{2,22},{4,16},{6,18},{8,28},{10,30},{12,24},{14,26},{16,4},... | collective-permute-start | bytes 208904 | tf_op jit(solution)/shard_map/ppermute | solution.py:291
  45.0 8.3 %collective-permute-start.14 = (bf16[2,8,2176]{2,1,0:T(8,128)(2,1)S(1)}, bf16[2,8,2176]{2,1,0:T(8,128)(2,1)S(1)}, u32[]{:S(2)}, u32[]{:S(2)}) collective-permute-start(bf16[2,8,2176]{2,1,0:T(8,128)(2,1)S(1)} %get-tuple-element.39), channel_id=1, source_target_pairs={{0,24},{2,26},{4,28},{6,30},{8,16},{10,18},{12,20},{14,22},{16,8},... | collective-permute-start | bytes 208904 | tf_op jit(solution)/shard_map/ppermute | solution.py:291
  47.9 7.1 %collective-permute-start.15 = (bf16[2,8,2176]{2,1,0:T(8,128)(2,1)S(1)}, bf16[2,8,2176]{2,1,0:T(8,128)(2,1)S(1)}, u32[]{:S(2)}, u32[]{:S(2)}) collective-permute-start(bf16[2,8,2176]{2,1,0:T(8,128)(2,1)S(1)} %get-tuple-element.40), channel_id=1, source_target_pairs={{0,28},{2,30},{4,24},{6,26},{8,20},{10,22},{12,16},{14,18},{16,12}... | collective-permute-start | bytes 208904 | tf_op jit(solution)/shard_map/ppermute | solution.py:291
  55.6 1.3 %collective-permute-start.16 = (bf16[8,2176]{1,0:T(8,128)(2,1)S(1)}, bf16[8,2176]{1,0:T(8,128)(2,1)S(1)}, u32[]{:S(2)}, u32[]{:S(2)}) collective-permute-start(bf16[8,2176]{1,0:T(8,128)(2,1)S(1)} %get-tuple-element.42), channel_id=1, source_target_pairs={{0,2},{2,0},{4,6},{6,4},{8,10},{10,8},{12,14},{14,12},{16,18},{18,... | collective-permute-start | bytes 104456 | tf_op jit(solution)/shard_map/ppermute | solution.py:291
  63.2 4.3 %collective-permute-start.17 = (f32[8,2048]{1,0:T(8,128)S(1)}, f32[8,2048]{1,0:T(8,128)S(1)}, u32[]{:S(2)}, u32[]{:S(2)}) collective-permute-start(f32[8,2048]{1,0:T(8,128)S(1)} %get-tuple-element.54), channel_id=1, source_target_pairs={{0,1},{1,0},{2,3},{3,2},{4,5},{5,4},{6,7},{7,6},{8,9},{9,8},{10,11... | collective-permute-start | bytes 196616 | tf_op jit(solution)/shard_map/ppermute | solution.py:428

commit v2 on v1

v2 whole, which is shorter than its diff:
```python
import functools

import jax
import jax.numpy as jnp
from jax import lax
from jax.experimental import pallas as pl
from jax.experimental.pallas import tpu as pltpu
from jax.sharding import PartitionSpec as P


HD = 128
PAGE = 64
LOG2E = 1.4426950408889634
VMEM = pltpu.VMEM
SMEM = pltpu.SMEM


def vmem_spec():
    return pl.BlockSpec(memory_space=VMEM)


def smem_spec():
    return pl.BlockSpec(memory_space=SMEM)


def hbm_spec():
    return pl.BlockSpec(memory_space=pltpu.HBM)


def in_hbm(x):
    return pltpu.with_memory_space_constraint(x, pltpu.HBM)


def place():
    return lax.axis_index("dp").astype(jnp.int32)


def split_kernel(half, q_ref, mine, other):
    core = lax.rem(place(), 2)
    mine[...] = q_ref[:, pl.ds(pl.multiple_of(core * half, 128), half)]
    other[...] = q_ref[:, pl.ds(pl.multiple_of((1 - core) * half, 128), half)]


def pair_kernel(mine, got, after, out):
    out[0] = mine[...]
    out[1] = got[...]


def share_kernel(cols, kv, after, out, sem):
    side = 1 - lax.rem(place(), 2) if kv.shape[2] > cols else 0
    copy = pltpu.make_async_copy(kv.at[:, :, pl.ds(pl.multiple_of(side * cols, 128), cols)], out, sem)
    copy.start()
    copy.wait()


def w_copies(plan, first, w, outs, sems):
    n_tp, chunk, width = plan
    per_chunk = chunk // width
    my_tp = lax.axis_index("tp").astype(jnp.int32)
    copies = []
    for i in range(outs.shape[0]):
        which, block = divmod(first + i, per_chunk)
        col = jnp.bitwise_xor(my_tp, (which + 1) % n_tp) * chunk + block * width
        copies.append(pltpu.make_async_copy(w.at[:, pl.ds(pl.multiple_of(col, 128), width)], outs.at[i], sems.at[i]))
    return copies


def load_kernel(plan, w, after, out, token, sems):
    copies = w_copies(plan, 0, w, out, sems)
    for copy in copies:
        copy.start()
    for copy in copies:
        copy.wait()
    token[...] = jnp.zeros_like(token)


def choose_kernel(chips, owner, *refs):
    parts, near, far = refs[:chips], refs[chips + 1], refs[chips + 2]
    source = jnp.bitwise_xor(place() // 2, owner[0] // 2)
    for d in range(chips):

        @pl.when(source == d)
        def _():
            near[...] = parts[d][0]
            far[...] = parts[d][1]


def resident_kernel(
    rows, groups, group, maxpages, table, lengths, q_ref, cache, out, lse_out, kbuf, vbuf, sems
):
    length = maxpages * PAGE
    scale = 1.0 / HD**0.5
    for kind, buf in ((0, kbuf), (1, vbuf)):
        for b in range(rows):
            for t in range(maxpages):
                pltpu.make_async_copy(
                    cache.at[kind, table[b * maxpages + t]], buf.at[b, t], sems.at[kind, b]
                ).start()
    m_rows = group * rows
    row_b = lax.rem(lax.broadcasted_iota(jnp.int32, (m_rows, 1), 0), rows)
    lens = jnp.zeros((m_rows, 1), jnp.int32)
    for b in range(rows):
        lens = jnp.where(row_b == b, lengths[b], lens)
    inside = lax.broadcasted_iota(jnp.int32, (m_rows, length), 1) < lens
    half_heads = groups * group // 2
    lane = lax.broadcasted_iota(jnp.int32, (rows, 128), 1)
    lse_out[...] = jnp.zeros_like(lse_out)

    def arrived(kind, buf):
        for b in range(rows):
            pltpu.make_async_copy(cache.at[kind, pl.ds(0, maxpages)], buf.at[b], sems.at[kind, b]).wait()

    arrived(0, kbuf)

    @pl.loop(0, groups)
    def _(g):
        kv_cols = pl.ds(pl.multiple_of(g * HD, HD), HD)
        q_cols = pl.ds(pl.multiple_of(g * group * HD, group * HD), group * HD)
        q = q_ref[:, q_cols].astype(jnp.float32)
        q = jnp.concatenate([q[:, h * HD : (h + 1) * HD] for h in range(group)], axis=0).astype(jnp.bfloat16)
        s = None
        for b in range(rows):
            keys = kbuf[b, :, :, kv_cols].reshape(length, HD)
            sb = lax.dot_general(q, keys, (((1,), (1,)), ((), ())), preferred_element_type=jnp.float32)
            s = sb if s is None else jnp.where(row_b == b, sb, s)
        s = jnp.where(inside, s, -jnp.inf)
        top = jnp.max(s, axis=1, keepdims=True)
        p = jnp.exp2((s - top) * (scale * LOG2E))
        den = jnp.sum(p, axis=1, keepdims=True)
        p = p.astype(jnp.bfloat16)

        @pl.when(g == 0)
        def _():
            arrived(1, vbuf)

        o = None
        for b in range(rows):
            values = vbuf[b, :, :, kv_cols].reshape(length, HD)
            ob = jnp.dot(p, values, preferred_element_type=jnp.float32)
            o = ob if o is None else jnp.where(row_b == b, ob, o)
        o = o * (1.0 / den)
        lse = top * scale + jnp.log(den)
        for h in range(group):
            head = g * group + h
            side, hh = head // half_heads, lax.rem(head, half_heads)
            part = slice(h * rows, (h + 1) * rows)
            out[side, :, pl.ds(pl.multiple_of(hh * HD, HD), HD)] = o[part]
            lse_out[side] = jnp.where(lane == hh, lse[part], lse_out[side])


def prefix_kernel(chips, rows, groups, group, n_readers, block, owner_ref, readers, *refs):
    q_refs = refs[:chips]
    own_kv, mate_kv = refs[chips : chips + 2]
    outs = refs[chips + 2 : 2 * chips + 2]
    keys, values, q_all, q_rows, o_rows, lse_rows, o_all, kv_sems = refs[2 * chips + 2 :]
    me, owner = place(), owner_ref[0]
    scale = 1.0 / HD**0.5
    half = groups * group * HD
    cols = groups * HD
    part = lax.rem(me, 2) if own_kv.shape[2] > cols else 0

    @pl.when(me // 2 == owner // 2)
    def _():
        for kind, buf in ((0, keys), (1, values)):

            @pl.when(me == owner)
            def _():
                own_part = own_kv.at[kind, :, pl.ds(pl.multiple_of(part * cols, 128), cols)]
                pltpu.make_async_copy(own_part, buf, kv_sems.at[kind]).start()

            @pl.when(me != owner)
            def _():
                pltpu.make_async_copy(mate_kv.at[kind], buf, kv_sems.at[kind]).start()

        for d in range(chips):
            for s in range(2):
                q_all[2 * d + s] = q_refs[d][s].astype(jnp.float32)
        for j in range(n_readers):
            slot = jnp.bitwise_xor(readers[j], me)
            x = q_all[slot]
            for g in range(groups):
                for h in range(group):
                    first = (h * n_readers + j) * rows
                    col = (g * group + h) * HD
                    q_rows[g, first : first + rows, :] = x[:, col : col + HD]
        total = group * n_readers * rows
        blocks = total // block

        for kind, buf in ((0, keys), (1, values)):
            pltpu.make_async_copy(mate_kv.at[kind], buf, kv_sems.at[kind]).wait()
        for g in range(groups):

            @pl.loop(0, blocks)
            def _(i):
                part = pl.ds(pl.multiple_of(i * block, block), block)
                q = q_rows[g, part, :].astype(jnp.bfloat16)
                k = keys[:, g * HD : (g + 1) * HD]
                s = lax.dot_general(q, k, (((1,), (1,)), ((), ())), preferred_element_type=jnp.float32)
                top = jnp.max(s, axis=1, keepdims=True)
                p = jnp.exp2((s - top) * (scale * LOG2E))
                den = jnp.sum(p, axis=1, keepdims=True)
                v = values[:, g * HD : (g + 1) * HD]
                o = jnp.dot(p.astype(jnp.bfloat16), v, preferred_element_type=jnp.float32)
                o_rows[g, part, :] = o * (1.0 / den)
                lse_rows[g, part, :] = jnp.broadcast_to(top * scale + jnp.log(den), (block, 128))

        lane = lax.broadcasted_iota(jnp.int32, (rows, 128), 1)
        heads = groups * group
        for j in range(n_readers):
            slot = jnp.bitwise_xor(readers[j], me)
            stat = jnp.zeros((rows, 128), jnp.float32)
            for g in range(groups):
                for h in range(group):
                    first = (h * n_readers + j) * rows
                    hh = g * group + h
                    o_all[slot, :, hh * HD : (hh + 1) * HD] = o_rows[g, first : first + rows, :]
                    val = lse_rows[g, first : first + rows, :]
                    top = val.astype(jnp.bfloat16).astype(jnp.float32)
                    rest = val - top
                    mid = rest.astype(jnp.bfloat16).astype(jnp.float32)
                    stat = jnp.where(lane == hh, top, stat)
                    stat = jnp.where(lane == heads + hh, mid, stat)
                    stat = jnp.where(lane == 2 * heads + hh, rest - mid, stat)
            o_all[slot, :, half:] = stat
        for d in range(chips):
            for s in range(2):
                outs[d][s] = o_all[2 * d + s].astype(jnp.bfloat16)


def project(attn, w, first, count, out, col):
    width = w.shape[2]

    @pl.loop(0, count)
    def _(j):
        cols = pl.ds(pl.multiple_of(col + j * width, width), width)
        out[:, cols] = jnp.dot(attn[...], w[first + j], preferred_element_type=jnp.float32)


def away_kernel(heads, plan, readers, near, far, res, res_lse, w_hbm, w, *refs):
    n_tp, chunk, width = plan
    per_chunk = chunk // width
    outs, (attn, w_late, w_sems) = refs[: n_tp - 1], refs[n_tp - 1 :]
    copies = w_copies(plan, n_tp * per_chunk - w_late.shape[0], w_hbm, w_late, w_sems)
    for copy in copies:
        copy.start()
    me = place()
    core = lax.rem(me, 2)
    is_reader = jnp.int32(0)
    for j in range(readers.shape[0]):
        is_reader = jnp.where(readers[j] == me, 1, is_reader)
    half = heads * HD
    for side in range(2):
        mine = core == side
        stat = jnp.where(mine, near[:, half:].astype(jnp.float32), far[:, half:].astype(jnp.float32))
        pre = stat + pltpu.roll(stat, 128 - heads, 1) + pltpu.roll(stat, 128 - 2 * heads, 1)
        weights = 1.0 / (1.0 + jnp.exp(res_lse[side] - pre))
        for h in range(heads):
            weight = weights[:, h : h + 1]
            cols = slice(h * HD, (h + 1) * HD)
            r = res[side, :, cols]
            x = jnp.where(mine, near[:, cols].astype(jnp.float32), far[:, cols].astype(jnp.float32))
            y = jnp.where(is_reader > 0, r + weight * (x - r), r)
            attn[:, side * half + h * HD : side * half + (h + 1) * HD] = y.astype(jnp.bfloat16)
    for i, out in enumerate(outs):
        project(attn, w, i * per_chunk, per_chunk, out, 0)
    for copy in copies:
        copy.wait()


def home_kernel(attn, w, w_late, out):
    late = w_late.shape[0]
    early = out.shape[1] // w.shape[2] - late
    if early:
        project(attn, w, w.shape[0] - early, early, out, 0)
    project(attn, w_late, 0, late, out, early * w.shape[2])


def shards(n_dp, n_tp, queries, prefix_kv, cache_kv, lengths, page_table, owner, readers, w_out):
    rows = queries.shape[0]
    heads = queries.shape[1] // HD
    groups = prefix_kv.shape[2] // HD
    group = heads // groups
    prefix = prefix_kv.shape[1]
    maxpages = page_table.shape[1] // rows
    n_readers = readers.shape[0]
    chips = n_dp // 2
    half_groups = max(groups // 2, 1)
    half_heads = heads // 2
    share_group = half_heads // half_groups
    half = half_heads * HD
    wide = half + 128
    d_out = w_out.shape[1]
    chunk = d_out // n_tp

    def hop(x, d):
        return lax.ppermute(x, "dp", [(i, i ^ d) for i in range(n_dp)])

    mine, other = pl.pallas_call(
        functools.partial(split_kernel, half),
        out_shape=tuple(jax.ShapeDtypeStruct((rows, half), jnp.bfloat16) for _ in range(2)),
        in_specs=[vmem_spec()],
        out_specs=(vmem_spec(), vmem_spec()),
        compiler_params=pltpu.CompilerParams(vmem_limit_bytes=2 << 20),
        name="split",
    )(queries)
    got = hop(other, 1)
    kv_cols = half_groups * HD
    shared = pl.pallas_call(
        functools.partial(share_kernel, kv_cols),
        out_shape=jax.ShapeDtypeStruct((2, prefix, kv_cols), jnp.bfloat16),
        in_specs=[hbm_spec(), vmem_spec()],
        out_specs=vmem_spec(),
        scratch_shapes=[pltpu.SemaphoreType.DMA(())],
        compiler_params=pltpu.CompilerParams(vmem_limit_bytes=4 << 20),
        cost_estimate=pl.CostEstimate(flops=1 << 24, bytes_accessed=4 * prefix * kv_cols, transcendentals=0),
        name="share",
    )(in_hbm(prefix_kv), other)
    pair = pl.pallas_call(
        pair_kernel,
        out_shape=jax.ShapeDtypeStruct((2, rows, half), jnp.bfloat16),
        in_specs=[vmem_spec()] * 3,
        out_specs=vmem_spec(),
        compiler_params=pltpu.CompilerParams(vmem_limit_bytes=2 << 20),
        cost_estimate=pl.CostEstimate(flops=1 << 32, bytes_accessed=1 << 24, transcendentals=0),
        name="pair",
    )(mine, got, shared)
    width = min(512, chunk)
    plan = (n_tp, chunk, width)
    last = min(3, chunk // width)
    counts = (d_out // width - last, last)

    def w_blocks(n):
        return VMEM((n, w_out.shape[0], width), w_out.dtype)

    def with_chip(x, root, d):
        if root is None:
            return hop(x, 2 * d)
        pairs = []
        for i in range(n_dp):
            far = i ^ (2 * d)
            pairs.append((i, far if root in (i // 2, far // 2) else i ^ 1))
        return lax.ppermute(x, "dp", pairs)

    def gather(root, pair, shared, table, lengths, queries, cache_kv):
        got = [with_chip(pair, root, d) for d in range(1, chips)]
        mate_kv = hop(shared, 1)
        res, res_lse = pl.pallas_call(
            functools.partial(resident_kernel, rows, groups, group, maxpages),
            out_shape=(
                jax.ShapeDtypeStruct((2, rows, half), jnp.float32),
                jax.ShapeDtypeStruct((2, rows, 128), jnp.float32),
            ),
            in_specs=[smem_spec(), smem_spec(), vmem_spec(), hbm_spec()],
            out_specs=(vmem_spec(), vmem_spec()),
            scratch_shapes=[
                VMEM((rows, maxpages, PAGE, groups * HD), jnp.bfloat16),
                VMEM((rows, maxpages, PAGE, groups * HD), jnp.bfloat16),
                pltpu.SemaphoreType.DMA((2, rows)),
            ],
            compiler_params=pltpu.CompilerParams(vmem_limit_bytes=13 << 20),
            cost_estimate=pl.CostEstimate(
                flops=4 * heads * rows * rows * maxpages * PAGE * HD,
                bytes_accessed=2 * rows * maxpages * PAGE * groups * HD * 2,
                transcendentals=heads * rows * maxpages * PAGE,
            ),
            name="resident",
        )(table, lengths, queries, in_hbm(cache_kv))
        return (*got, mate_kv, res, res_lse)

    def finish(root, w_out, owner, readers, res, res_lse, *pre):
        back = [pre[0]] + [with_chip(pre[d], root, d) for d in range(1, chips)]
        loaded, token = pl.pallas_call(
            functools.partial(load_kernel, plan),
            out_shape=(w_blocks(counts[0]), jax.ShapeDtypeStruct((8, 128), jnp.float32)),
            in_specs=[hbm_spec(), vmem_spec()],
            out_specs=(vmem_spec(), vmem_spec()),
            scratch_shapes=[pltpu.SemaphoreType.DMA((counts[0],))],
            compiler_params=pltpu.CompilerParams(vmem_limit_bytes=2 << 20),
            cost_estimate=pl.CostEstimate(flops=1 << 28, bytes_accessed=w_out.size, transcendentals=0),
            name="load",
        )(in_hbm(w_out), pre[0])
        near, other = pl.pallas_call(
            functools.partial(choose_kernel, chips),
            out_shape=tuple(jax.ShapeDtypeStruct((rows, wide), jnp.bfloat16) for _ in range(2)),
            in_specs=[smem_spec()] + [vmem_spec()] * (chips + 1),
            out_specs=(vmem_spec(), vmem_spec()),
            compiler_params=pltpu.CompilerParams(vmem_limit_bytes=4 << 20),
            name="choose",
        )(owner, *back, token)
        far = hop(other, 1)
        in_vmem = functools.partial(pltpu.with_memory_space_constraint, memory_space=VMEM)
        cost = pl.CostEstimate(
            flops=2 * rows * heads * HD * chunk * 16, bytes_accessed=2 * heads * HD * chunk, transcendentals=0
        )
        *away, attn, late = pl.pallas_call(
            functools.partial(away_kernel, half_heads, plan),
            out_shape=tuple(jax.ShapeDtypeStruct((rows, chunk), jnp.float32) for _ in range(n_tp - 1))
            + (jax.ShapeDtypeStruct((rows, heads * HD), jnp.bfloat16), w_blocks(counts[1])),
            in_specs=[smem_spec()] + [vmem_spec()] * 4 + [hbm_spec(), vmem_spec()],
            out_specs=(vmem_spec(),) * (n_tp + 1),
            scratch_shapes=[pltpu.SemaphoreType.DMA((counts[1],))],
            compiler_params=pltpu.CompilerParams(vmem_limit_bytes=4 << 20),
            cost_estimate=cost,
            name="away",
        )(readers, near, far, res, res_lse, in_hbm(w_out), in_vmem(loaded))
        home = pl.pallas_call(
            home_kernel,
            out_shape=jax.ShapeDtypeStruct((rows, chunk), jnp.float32),
            in_specs=[vmem_spec()] * 3,
            out_specs=vmem_spec(),
            compiler_params=pltpu.CompilerParams(vmem_limit_bytes=4 << 20),
            cost_estimate=cost,
            name="home",
        )(attn, in_vmem(loaded), in_vmem(late))
        for k in range(1, n_tp):
            home = home + lax.ppermute(away[k - 1], "tp", [(i, i ^ k) for i in range(n_tp)])
        return home.astype(jnp.bfloat16)

    def routed(step, *operands):
        if chips > 8:
            return step(None, *operands)
        return lax.switch(owner[0] // 2, [functools.partial(step, k) for k in range(chips)], *operands)

    *gathered, mate_kv, res, res_lse = routed(gather, pair, shared, page_table[0], lengths, queries, cache_kv)
    gathered = [pair] + gathered
    total = share_group * n_readers * rows
    block = min(256, total)
    pre = pl.pallas_call(
        functools.partial(prefix_kernel, chips, rows, half_groups, share_group, n_readers, block),
        out_shape=tuple(jax.ShapeDtypeStruct((2, rows, wide), jnp.bfloat16) for _ in range(chips)),
        in_specs=[smem_spec(), smem_spec()] + [vmem_spec()] * chips + [hbm_spec()] * 2,
        out_specs=(vmem_spec(),) * chips,
        scratch_shapes=[
            VMEM((prefix, kv_cols), jnp.bfloat16),
            VMEM((prefix, kv_cols), jnp.bfloat16),
            VMEM((2 * chips, rows, half), jnp.float32),
            VMEM((half_groups, total, HD), jnp.float32),
            VMEM((half_groups, total, HD), jnp.float32),
            VMEM((half_groups, total, 128), jnp.float32),
            VMEM((2 * chips, rows, wide), jnp.float32),
            pltpu.SemaphoreType.DMA((2,)),
        ],
        compiler_params=pltpu.CompilerParams(vmem_limit_bytes=16 << 20),
        cost_estimate=pl.CostEstimate(
            flops=4 * half_groups * total * prefix * HD,
            bytes_accessed=4 * half_groups * prefix * HD,
            transcendentals=half_groups * total * prefix,
        ),
        name="prefix",
    )(owner, readers, *gathered, in_hbm(prefix_kv), in_hbm(mate_kv))
    return routed(finish, w_out, owner, readers, res, res_lse, *pre)


def solution(mesh):
    placed = (
        P("dp", "tp"),
        P(None, "dp", "tp"),
        P(None, "dp", None, "tp"),
        P("dp"),
        P("dp", None),
        P(),
        P(),
        P("tp", None),
    )
    return jax.shard_map(
        functools.partial(shards, mesh.shape["dp"], mesh.shape["tp"]),
        mesh=mesh,
        in_specs=placed,
        out_specs=P("dp", "tp"),
        check_vma=False,
    )
```

time: 68.3 us -> 60.9 us (0.89)
  waiting for transfers between devices: 11.8 us -> 3.91 us
  starting transfers between devices: 30.1 us -> 26.4 us
  between operations: 0.14 us -> 2.72 us
  Pallas kernels: 24.7 us -> 26.5 us
    ppermute x17 -> x3, starting transfers between devices: 28.5 us -> 0.65 us  [hop(): return lax.ppermute(x, 'dp', [(i, i ^ d) for i in range(n_dp)])]
    ppermute x1 -> x15, starting transfers between devices: 1.58 us -> 25.8 us  [the longest x14 24.2 us: with_chip(): return lax.ppermute(x, 'dp', pairs)]
    ppermute x17 -> x3, waiting for transfers between devices: 11.3 us -> 1.2 us  [hop(): return lax.ppermute(x, 'dp', [(i, i ^ d) for i in range(n_dp)])]
    pallas_call x4 -> x5, Pallas kernels: 15.3 us -> 22.9 us  [the longest x1 7.26 us: gather(): pl.pallas_call(functools.partial(resident_kernel, rows, groups, group, ma...]
    pallas_call x1, Pallas kernels: 7.73 us -> 1.09 us  [shards(): pl.pallas_call(functools.partial(prefix_kernel, chips, rows, half_groups,...]
    ppermute x1 -> x15, waiting for transfers between devices: 0.48 us -> 2.7 us  [the longest x14 2.57 us: with_chip(): return lax.ppermute(x, 'dp', pairs)]
    pallas_call x1, Pallas kernels: 0.01 us -> 0.91 us  [shards(): pl.pallas_call(functools.partial(split_kernel, half), out_shape=tuple((ja...]
  transfers between devices with their start and end apart: 18 -> 18, of which waited for: 8 -> 3; matrix products, arithmetic and copies ran while one was open for 0% -> 0% of each run, Pallas kernels for 12% -> 31%
where the time goes in v2:
time: 60.9 us; the launch traced here: 60.6 us
  Pallas kernels  26.5 us (44%)
  starting transfers between devices  26.4 us (43%)
  waiting for transfers between devices  3.91 us (6%)
  between operations  2.72 us (4%)
  local copies, waits for them, and re-layouts  0.63 us (1%)
    ppermute x14, starting transfers between devices, with_chip(): return lax.ppermute(x, 'dp', pairs)  24.2 us
    pallas_call x1, Pallas kernels, gather(): pl.pallas_call(functools.partial(resident_kernel, rows, groups, group, ma...  7.26 us
    pallas_call x1, Pallas kernels, finish(): pl.pallas_call(functools.partial(load_kernel, plan), out_shape=(w_blocks(...  7.15 us
    pallas_call x1, Pallas kernels, finish(): pl.pallas_call(functools.partial(away_kernel, half_heads, plan), out_shap...  5.28 us
    pallas_call x1, Pallas kernels, finish(): pl.pallas_call(home_kernel, out_shape=jax.ShapeDtypeStruct((rows, chunk),...  2.61 us
    ppermute x14, waiting for transfers between devices, with_chip(): return lax.ppermute(x, 'dp', pairs)  2.57 us
    pallas_call x1, Pallas kernels, shards(): pl.pallas_call(functools.partial(share_kernel, kv_cols), out_shape=jax.Sh...  1.61 us
    ppermute x1, starting transfers between devices, finish(): lax.ppermute(away[k - 1], 'tp', [(i, i ^ k) for i in range(n_tp)])  1.58 us
  transfers between devices with their start and end apart: 18, of which 3 were waited for; matrix products, arithmetic and copies ran while one was open for 0% of the time, Pallas kernels for 31%

profile of v2, /device:TPU:0, one launch (start us, length us, event | category | flops | bytes accessed | tf_op | source)
XLA Modules:
  0.0 60.6 jit_solution(5225915832057409792)
XLA Ops:
  0.0 0.9 %split.1 = (bf16[8,2048]{1,0:T(8,128)(2,1)S(1)}, bf16[8,2048]{1,0:T(8,128)(2,1)S(1)}) custom-call(bf16[8,4096]{1,0:T(8,128)(2,1)} %q_ref.1), custom_call_target="tpu_custom_call" | custom-call | tf_op jit(solution)/shard_map/split/pallas_call | solution.py:298
  0.9 0.5 collective-permute-start.136
  4.0 1.6 %share.1.after = bf16[2,2048,256]{2,1,0:T(8,128)(2,1)S(1)} custom-call(bf16[2,2048,512]{2,1,0:T(8,128)(2,1)} %refs_8_.1, bf16[8,2048]{1,0:T(8,128)(2,1)S(1)} %get-tuple-element.569.after), custom_call_target="tpu_custom_call" | custom-call | flops 16777216 | bytes 2097152 | tf_op jit(solution)/shard_map/share/pallas_call | solution.py:308
  5.7 17.3 %conditional.4 = (bf16[2,8,2048]{2,1,0:T(8,128)(2,1)}, bf16[2,8,2048]{2,1,0:T(8,128)(2,1)}, bf16[2,8,2048]{2,1,0:T(8,128)(2,1)}, bf16[2,8,2048]{2,1,0:T(8,128)(2...) conditional(s32[]{:T(128)} %clamp.4, ...), branch_computations={%region_0.1_spmd, %region_1.2_spmd, %region_2.3_spmd, %region_3.4_... | conditional | flops 536870912 | bytes 18612624 | solution.py:422
  5.9 6.0 %collective-permute-start.62 = (bf16[2,8,2048]{2,1,0:T(8,128)(2,1)S(1)}, bf16[2,8,2048]{2,1,0:T(8,128)(2,1)}, u32[]{:S(2)}, u32[]{:S(2)}) collective-permute-start(bf16[2,8,2048]{2,1,0:T(8,128)(2,1)S(1)} %get-tuple-element.380), channel_id=1, source_target_pairs={{0,28},{2,30},{4,6},{6,4},{8,10},{10,8},{12,14},{14,12},{16,18},{1... | collective-permute-start | bytes 196616 | tf_op jit(solution)/shard_map/cond/branch_7_fun/ppermute | solution.py:342
  11.9 0.5 collective-permute-start.60
  12.4 2.5 %collective-permute-done.62 = bf16[2,8,2048]{2,1,0:T(8,128)(2,1)} collective-permute-done((bf16[2,8,2048]{2,1,0:T(8,128)(2,1)S(1)}, bf16[2,8,2048]{2,1,0:T(8,128)(2,1)}, u32[]{:S(2)}, u32[]{:S(2)}) %collective-permute-start.62) | collective-permute-done | bytes 65568 | tf_op jit(solution)/shard_map/cond/branch_7_fun/ppermute | solution.py:342
  14.9 0.5 collective-permute-start.57
  15.5 7.3 %resident.15 = (f32[2,8,2048]{2,1,0:T(8,128)S(1)}, f32[2,8,128]{2,1,0:T(8,128)S(1)}) custom-call(s32[64]{0:T(128)S(1)} %get-tuple-element.382.table, s32[8]{0:T(128)S(1)} %get-tuple-element.383.lengths, bf16[8,4096]{1,0:T(8,128)(2,1)S(1)} %get-tuple-element.384.q_ref, bf16[2,64,64,512]{3,2,1,0:T(8,128)(2,1)} %get-tuple-element.385.cache), custom_call_target="tpu_custom_call" | custom-call | flops 536870912 | bytes 8388608 | tf_op jit(solution)/shard_map/cond/branch_7_fun/resident/pallas_call | solution.py:347
  23.0 1.1 %prefix.1 = (bf16[2,8,2176]{2,1,0:T(8,128)(2,1)S(1)}, bf16[2,8,2176]{2,1,0:T(8,128)(2,1)S(1)}, bf16[2,8,2176]{2,1,0:T(8,128)(2,1)S(1)}, bf16[2,8,2176]{2,1,0:T(8...) custom-call(s32[16]{0:T(128)S(1)} %copy-done.1, ...), custom_call_target="tpu_custom_call" | custom-call | flops 1073741824 | bytes 2097152 | tf_op jit(solution)/shard_map/prefix/pallas_call | solution.py:428
  24.1 35.9 %conditional.6 = (bf16[8,2048]{1,0:T(8,128)(2,1)S(1)}) conditional(s32[]{:T(128)} %clamp.4, (bf16[2,8,2176]{2,1,0:T(8,128)(2,1)S(1)}, bf16[2,8,2176]{2,1,0:T(8,128)(2,1)S(1)}, bf16[2,8,2176]{2,1,0:T(8,128)(2,1)S(1)}, bf16[2,8,2176]{2,1,0:T(8,128)(2,1)S(1)}, bf16[2,8,2176]{2,1,0:T(8,128)(2,1)S(1)}, ...), branch_computations={%region_8.9_spmd, %region_9.10_spmd, %region_10.11_spmd, %region_1... | conditional | flops 4563419136 | bytes 52846960
  24.2 0.5 collective-permute-start.127
  24.7 0.4 collective-permute-start.129
  25.3 0.4 collective-permute-start.131
  25.7 0.2 collective-permute-start.132
  25.9 15.3 %collective-permute-start.133 = (bf16[2,8,2176]{2,1,0:T(8,128)(2,1)S(1)}, bf16[2,8,2176]{2,1,0:T(8,128)(2,1)S(1)}, u32[]{:S(2)}, u32[]{:S(2)}) collective-permute-start(bf16[2,8,2176]{2,1,0:T(8,128)(2,1)S(1)} %get-tuple-element.537), channel_id=1, source_target_pairs={{0,28},{2,30},{4,6},{6,4},{8,10},{10,8},{12,14},{14,12},{16,18},{1... | collective-permute-start | bytes 208904 | tf_op jit(solution)/shard_map/cond/branch_7_fun/ppermute | solution.py:342
  41.3 7.2 %load.15 = (bf16[5,4096,512]{2,1,0:T(8,128)(2,1)S(1)}, f32[8,128]{1,0:T(8,128)S(1)}) custom-call(bf16[4096,4096]{1,0:T(8,128)(2,1)} %get-tuple-element.538.w.w_hbm, bf16[2,8,2176]{2,1,0:T(8,128)(2,1)S(1)} %get-tuple-element.530.after.refs_0_), custom_call_target="tpu_custom_call" | custom-call | flops 268435456 | bytes 16777216 | tf_op jit(solution)/shard_map/cond/branch_7_fun/load/pallas_call | solution.py:372
  48.5 0.6 choose.15
  49.2 1.2 %collective-permute-done.134.far = bf16[8,2176]{1,0:T(8,128)(2,1)S(1)} collective-permute-done((bf16[8,2176]{1,0:T(8,128)(2,1)S(1)}, bf16[8,2176]{1,0:T(8,128)(2,1)S(1)}, u32[]{:S(2)}, u32[]{:S(2)}) %collective-permute-start.134) | collective-permute-done | bytes 34848 | tf_op jit(solution)/shard_map/cond/branch_7_fun/ppermute | solution.py:296
  50.4 5.3 %away.15 = (f32[8,2048]{1,0:T(8,128)S(1)}, bf16[8,4096]{1,0:T(8,128)(2,1)S(1)}, bf16[3,4096,512]{2,1,0:T(8,128)(2,1)S(1)}) custom-call(s32[8]{0:T(128)S(1)} %get-tuple-element.528.readers, bf16[8,2176]{1,0:T(8,128)(2,1)S(1)} %get-tuple-element.540.near, bf16[8,2176]{1,0:T(8,128)(2,1)S(1)} %collective-permute-done.134.far, ...), custom_call_target="tpu_custom_call" | custom-call | flops 2147483648 | bytes 16777216 | tf_op jit(solution)/shard_map/cond/branch_7_fun/away/pallas_call | solution.py:395
  55.7 1.6 %collective-permute-start.135 = (f32[8,2048]{1,0:T(8,128)S(1)}, f32[8,2048]{1,0:T(8,128)S(1)}, u32[]{:S(2)}, u32[]{:S(2)}) collective-permute-start(f32[8,2048]{1,0:T(8,128)S(1)} %get-tuple-element.547), channel_id=1, source_target_pairs={{0,1},{1,0},{2,3},{3,2},{4,5},{5,4},{6,7},{7,6},{8,9},{9,8},{10,11... | collective-permute-start | bytes 196616 | tf_op jit(solution)/shard_map/cond/branch_7_fun/ppermute | solution.py:416
  57.2 2.6 %home.15 = f32[8,2048]{1,0:T(8,128)S(1)} custom-call(bf16[8,4096]{1,0:T(8,128)(2,1)S(1)} %get-tuple-element.545.attn, bf16[5,4096,512]{2,1,0:T(8,128)(2,1)S(1)} %get-tuple-element.544.w, bf16[3,4096,512]{2,1,0:T(8,128)(2,1)S(1)} %get-tuple-element.546.w_late), custom_call_target="tpu_custom_call" | custom-call | flops 2147483648 | bytes 16777216 | tf_op jit(solution)/shard_map/cond/branch_7_fun/home/pallas_call | solution.py:406
  59.8 0.1 collective-permute-done.135
  60.0 0.6 copy-done.5
  (36 shorter events, 0.5 us)
Async XLA Ops:
  0.0 5.7 %copy-start = (bf16[8,4096]{1,0:T(8,128)(2,1)S(1)}, bf16[8,4096]{1,0:T(8,128)(2,1)}, u32[]{:S(2)}) copy-start(bf16[8,4096]{1,0:T(8,128)(2,1)} %q_ref.1) | copy-start | bytes 196612
  0.0 5.7 %copy-start.3 = (s32[1,64]{1,0:T(1,128)S(1)}, s32[1,64]{1,0:T(1,128)}, u32[]{:S(2)}) copy-start(s32[1,64]{1,0:T(1,128)} %param.28) | copy-start | bytes 772
  0.0 5.7 %copy-start.4 = (s32[8]{0:T(128)S(1)}, s32[8]{0:T(128)}, u32[]{:S(2)}) copy-start(s32[8]{0:T(128)} %param.27) | copy-start | bytes 100
  0.9 4.7 %collective-permute-start.136 = (bf16[8,2048]{1,0:T(8,128)(2,1)S(1)}, bf16[8,2048]{1,0:T(8,128)(2,1)S(1)}, u32[]{:S(2)}, u32[]{:S(2)}) collective-permute-start(bf16[8,2048]{1,0:T(8,128)(2,1)S(1)} %get-tuple-element.569.after), channel_id=1, source_target_pairs={{0,2},{2,0},{4,6},{6,4},{8,10},{10,8},{12,14},{14,12},{16,18},{18,... | collective-permute-start | bytes 98312 | tf_op jit(solution)/shard_map/ppermute | solution.py:296
  5.7 17.3 %copy-start.1 = (s32[16]{0:T(128)S(1)}, s32[16]{0:T(128)}, u32[]{:S(2)}) copy-start(s32[16]{0:T(128)} %owner_ref.1) | copy-start | bytes 196
  5.7 17.3 %copy-start.2 = (s32[8]{0:T(128)S(1)}, s32[8]{0:T(128)}, u32[]{:S(2)}) copy-start(s32[8]{0:T(128)} %readers.1) | copy-start | bytes 100
  5.8 17.0 %collective-permute-start.63 = (bf16[2,2048,256]{2,1,0:T(8,128)(2,1)S(1)}, bf16[2,2048,256]{2,1,0:T(8,128)(2,1)}, u32[]{:S(2)}, u32[]{:S(2)}) collective-permute-start(bf16[2,2048,256]{2,1,0:T(8,128)(2,1)S(1)} %get-tuple-element.381), channel_id=1, source_target_pairs={{0,2},{2,0},{4,6},{6,4},{8,10},{10,8},{12,14},{14,12},{16,18},{18,... | collective-permute-start | bytes 6291464 | tf_op jit(solution)/shard_map/cond/branch_7_fun/ppermute | solution.py:296
  5.9 9.1 %collective-permute-start.62 = (bf16[2,8,2048]{2,1,0:T(8,128)(2,1)S(1)}, bf16[2,8,2048]{2,1,0:T(8,128)(2,1)}, u32[]{:S(2)}, u32[]{:S(2)}) collective-permute-start(bf16[2,8,2048]{2,1,0:T(8,128)(2,1)S(1)} %get-tuple-element.380), channel_id=1, source_target_pairs={{0,28},{2,30},{4,6},{6,4},{8,10},{10,8},{12,14},{14,12},{16,18},{1... | collective-permute-start | bytes 196616 | tf_op jit(solution)/shard_map/cond/branch_7_fun/ppermute | solution.py:342
  11.9 3.1 %collective-permute-start.61 = (bf16[2,8,2048]{2,1,0:T(8,128)(2,1)S(1)}, bf16[2,8,2048]{2,1,0:T(8,128)(2,1)}, u32[]{:S(2)}, u32[]{:S(2)}) collective-permute-start(bf16[2,8,2048]{2,1,0:T(8,128)(2,1)S(1)} %get-tuple-element.380), channel_id=1, source_target_pairs={{0,2},{2,0},{4,28},{6,30},{8,10},{10,8},{12,14},{14,12},{16,18},{1... | collective-permute-start | bytes 196616 | tf_op jit(solution)/shard_map/cond/branch_7_fun/ppermute | solution.py:342
  11.9 3.6 %collective-permute-start.60 = (bf16[2,8,2048]{2,1,0:T(8,128)(2,1)S(1)}, bf16[2,8,2048]{2,1,0:T(8,128)(2,1)}, u32[]{:S(2)}, u32[]{:S(2)}) collective-permute-start(bf16[2,8,2048]{2,1,0:T(8,128)(2,1)S(1)} %get-tuple-element.380), channel_id=1, source_target_pairs={{0,2},{2,0},{4,6},{6,4},{8,28},{10,30},{12,14},{14,12},{16,18},{18... | collective-permute-start | bytes 196616 | tf_op jit(solution)/shard_map/cond/branch_7_fun/ppermute | solution.py:342
  12.4 10.4 %collective-permute-start.59 = (bf16[2,8,2048]{2,1,0:T(8,128)(2,1)S(1)}, bf16[2,8,2048]{2,1,0:T(8,128)(2,1)}, u32[]{:S(2)}, u32[]{:S(2)}) collective-permute-start(bf16[2,8,2048]{2,1,0:T(8,128)(2,1)S(1)} %get-tuple-element.380), channel_id=1, source_target_pairs={{0,2},{2,0},{4,6},{6,4},{8,10},{10,8},{12,28},{14,30},{16,18},{18,... | collective-permute-start | bytes 196616 | tf_op jit(solution)/shard_map/cond/branch_7_fun/ppermute | solution.py:342
  14.9 7.9 %collective-permute-start.58 = (bf16[2,8,2048]{2,1,0:T(8,128)(2,1)S(1)}, bf16[2,8,2048]{2,1,0:T(8,128)(2,1)}, u32[]{:S(2)}, u32[]{:S(2)}) collective-permute-start(bf16[2,8,2048]{2,1,0:T(8,128)(2,1)S(1)} %get-tuple-element.380), channel_id=1, source_target_pairs={{0,2},{2,0},{4,6},{6,4},{8,10},{10,8},{12,14},{14,12},{16,28},{18,... | collective-permute-start | bytes 196616 | tf_op jit(solution)/shard_map/cond/branch_7_fun/ppermute | solution.py:342
  14.9 7.9 %collective-permute-start.57 = (bf16[2,8,2048]{2,1,0:T(8,128)(2,1)S(1)}, bf16[2,8,2048]{2,1,0:T(8,128)(2,1)}, u32[]{:S(2)}, u32[]{:S(2)}) collective-permute-start(bf16[2,8,2048]{2,1,0:T(8,128)(2,1)S(1)} %get-tuple-element.380), channel_id=1, source_target_pairs={{0,2},{2,0},{4,6},{6,4},{8,10},{10,8},{12,14},{14,12},{16,18},{18,... | collective-permute-start | bytes 196616 | tf_op jit(solution)/shard_map/cond/branch_7_fun/ppermute | solution.py:342
  15.4 7.4 %collective-permute-start.56 = (bf16[2,8,2048]{2,1,0:T(8,128)(2,1)S(1)}, bf16[2,8,2048]{2,1,0:T(8,128)(2,1)}, u32[]{:S(2)}, u32[]{:S(2)}) collective-permute-start(bf16[2,8,2048]{2,1,0:T(8,128)(2,1)S(1)} %get-tuple-element.380), channel_id=1, source_target_pairs={{0,2},{2,0},{4,6},{6,4},{8,10},{10,8},{12,14},{14,12},{16,18},{18,... | collective-permute-start | bytes 196616 | tf_op jit(solution)/shard_map/cond/branch_7_fun/ppermute | solution.py:342
  24.2 1.5 %collective-permute-start.127 = (bf16[2,8,2176]{2,1,0:T(8,128)(2,1)S(1)}, bf16[2,8,2176]{2,1,0:T(8,128)(2,1)S(1)}, u32[]{:S(2)}, u32[]{:S(2)}) collective-permute-start(bf16[2,8,2176]{2,1,0:T(8,128)(2,1)S(1)} %get-tuple-element.531), channel_id=1, source_target_pairs={{0,2},{2,0},{4,6},{6,4},{8,10},{10,8},{12,14},{14,12},{16,18},{18,... | collective-permute-start | bytes 208904 | tf_op jit(solution)/shard_map/cond/branch_7_fun/ppermute | solution.py:342
  24.7 1.3 %collective-permute-start.128 = (bf16[2,8,2176]{2,1,0:T(8,128)(2,1)S(1)}, bf16[2,8,2176]{2,1,0:T(8,128)(2,1)S(1)}, u32[]{:S(2)}, u32[]{:S(2)}) collective-permute-start(bf16[2,8,2176]{2,1,0:T(8,128)(2,1)S(1)} %get-tuple-element.532), channel_id=1, source_target_pairs={{0,2},{2,0},{4,6},{6,4},{8,10},{10,8},{12,14},{14,12},{16,18},{18,... | collective-permute-start | bytes 208904 | tf_op jit(solution)/shard_map/cond/branch_7_fun/ppermute | solution.py:342
  24.7 23.7 %collective-permute-start.129 = (bf16[2,8,2176]{2,1,0:T(8,128)(2,1)S(1)}, bf16[2,8,2176]{2,1,0:T(8,128)(2,1)S(1)}, u32[]{:S(2)}, u32[]{:S(2)}) collective-permute-start(bf16[2,8,2176]{2,1,0:T(8,128)(2,1)S(1)} %get-tuple-element.533), channel_id=1, source_target_pairs={{0,2},{2,0},{4,6},{6,4},{8,10},{10,8},{12,14},{14,12},{16,28},{18,... | collective-permute-start | bytes 208904 | tf_op jit(solution)/shard_map/cond/branch_7_fun/ppermute | solution.py:342
  25.2 23.3 %collective-permute-start.130 = (bf16[2,8,2176]{2,1,0:T(8,128)(2,1)S(1)}, bf16[2,8,2176]{2,1,0:T(8,128)(2,1)S(1)}, u32[]{:S(2)}, u32[]{:S(2)}) collective-permute-start(bf16[2,8,2176]{2,1,0:T(8,128)(2,1)S(1)} %get-tuple-element.534), channel_id=1, source_target_pairs={{0,2},{2,0},{4,6},{6,4},{8,10},{10,8},{12,28},{14,30},{16,18},{18,... | collective-permute-start | bytes 208904 | tf_op jit(solution)/shard_map/cond/branch_7_fun/ppermute | solution.py:342
  25.3 23.2 %collective-permute-start.131 = (bf16[2,8,2176]{2,1,0:T(8,128)(2,1)S(1)}, bf16[2,8,2176]{2,1,0:T(8,128)(2,1)S(1)}, u32[]{:S(2)}, u32[]{:S(2)}) collective-permute-start(bf16[2,8,2176]{2,1,0:T(8,128)(2,1)S(1)} %get-tuple-element.535), channel_id=1, source_target_pairs={{0,2},{2,0},{4,6},{6,4},{8,28},{10,30},{12,14},{14,12},{16,18},{18... | collective-permute-start | bytes 208904 | tf_op jit(solution)/shard_map/cond/branch_7_fun/ppermute | solution.py:342
  25.7 22.8 %collective-permute-start.132 = (bf16[2,8,2176]{2,1,0:T(8,128)(2,1)S(1)}, bf16[2,8,2176]{2,1,0:T(8,128)(2,1)S(1)}, u32[]{:S(2)}, u32[]{:S(2)}) collective-permute-start(bf16[2,8,2176]{2,1,0:T(8,128)(2,1)S(1)} %get-tuple-element.536), channel_id=1, source_target_pairs={{0,2},{2,0},{4,28},{6,30},{8,10},{10,8},{12,14},{14,12},{16,18},{1... | collective-permute-start | bytes 208904 | tf_op jit(solution)/shard_map/cond/branch_7_fun/ppermute | solution.py:342
  25.9 22.6 %collective-permute-start.133 = (bf16[2,8,2176]{2,1,0:T(8,128)(2,1)S(1)}, bf16[2,8,2176]{2,1,0:T(8,128)(2,1)S(1)}, u32[]{:S(2)}, u32[]{:S(2)}) collective-permute-start(bf16[2,8,2176]{2,1,0:T(8,128)(2,1)S(1)} %get-tuple-element.537), channel_id=1, source_target_pairs={{0,28},{2,30},{4,6},{6,4},{8,10},{10,8},{12,14},{14,12},{16,18},{1... | collective-permute-start | bytes 208904 | tf_op jit(solution)/shard_map/cond/branch_7_fun/ppermute | solution.py:342
  49.1 1.3 %collective-permute-start.134 = (bf16[8,2176]{1,0:T(8,128)(2,1)S(1)}, bf16[8,2176]{1,0:T(8,128)(2,1)S(1)}, u32[]{:S(2)}, u32[]{:S(2)}) collective-permute-start(bf16[8,2176]{1,0:T(8,128)(2,1)S(1)} %get-tuple-element.541), channel_id=1, source_target_pairs={{0,2},{2,0},{4,6},{6,4},{8,10},{10,8},{12,14},{14,12},{16,18},{18,... | collective-permute-start | bytes 104456 | tf_op jit(solution)/shard_map/cond/branch_7_fun/ppermute | solution.py:296
  55.7 4.3 %collective-permute-start.135 = (f32[8,2048]{1,0:T(8,128)S(1)}, f32[8,2048]{1,0:T(8,128)S(1)}, u32[]{:S(2)}, u32[]{:S(2)}) collective-permute-start(f32[8,2048]{1,0:T(8,128)S(1)} %get-tuple-element.547), channel_id=1, source_target_pairs={{0,1},{1,0},{2,3},{3,2},{4,5},{5,4},{6,7},{7,6},{8,9},{9,8},{10,11... | collective-permute-start | bytes 196616 | tf_op jit(solution)/shard_map/cond/branch_7_fun/ppermute | solution.py:416
  60.0 0.6 %copy-start.5 = (bf16[8,2048]{1,0:T(8,128)(2,1)}, bf16[8,2048]{1,0:T(8,128)(2,1)S(1)}, u32[]{:S(2)}) copy-start(bf16[8,2048]{1,0:T(8,128)(2,1)S(1)} %get-tuple-element.833) | copy-start | bytes 98308

commit v3 on v2

--- a/solution.py
+++ b/solution.py
@@ -35,7 +35,8 @@
     return lax.axis_index("dp").astype(jnp.int32)
 
 
-def split_kernel(half, q_ref, mine, other):
+def split_kernel(half, q_ref, mine, other, whole):
+    whole[...] = q_ref[...]
     core = lax.rem(place(), 2)
     mine[...] = q_ref[:, pl.ds(pl.multiple_of(core * half, 128), half)]
     other[...] = q_ref[:, pl.ds(pl.multiple_of((1 - core) * half, 128), half)]
@@ -74,9 +75,11 @@
     token[...] = jnp.zeros_like(token)
 
 
-def choose_kernel(chips, owner, *refs):
+def choose_kernel(chips, root, *refs):
+    if root is None:
+        root, refs = refs[-3][0] // 2, refs[:-3] + refs[-2:]
     parts, near, far = refs[:chips], refs[chips + 1], refs[chips + 2]
-    source = jnp.bitwise_xor(place() // 2, owner[0] // 2)
+    source = jnp.bitwise_xor(place() // 2, root)
     for d in range(chips):
 
         @pl.when(source == d)
@@ -152,7 +155,7 @@
     q_refs = refs[:chips]
     own_kv, mate_kv = refs[chips : chips + 2]
     outs = refs[chips + 2 : 2 * chips + 2]
-    keys, values, q_all, q_rows, o_rows, lse_rows, o_all, kv_sems = refs[2 * chips + 2 :]
+    keys, values, q_in, q_rows, o_rows, lse_rows, o_all, kv_sems, q_sems = refs[2 * chips + 2 :]
     me, owner = place(), owner_ref[0]
     scale = 1.0 / HD**0.5
     half = groups * group * HD
@@ -161,7 +164,11 @@
 
     @pl.when(me // 2 == owner // 2)
     def _():
+        q_copies = [pltpu.make_async_copy(q_refs[d], q_in.at[d], q_sems.at[d]) for d in range(1, chips)]
         for kind, buf in ((0, keys), (1, values)):
+            if kind:
+                for copy in q_copies:
+                    copy.start()
 
             @pl.when(me == owner)
             def _():
@@ -172,12 +179,12 @@
             def _():
                 pltpu.make_async_copy(mate_kv.at[kind], buf, kv_sems.at[kind]).start()
 
-        for d in range(chips):
-            for s in range(2):
-                q_all[2 * d + s] = q_refs[d][s].astype(jnp.float32)
+        q_in[0] = q_refs[0][...]
+        for copy in q_copies:
+            copy.wait()
         for j in range(n_readers):
             slot = jnp.bitwise_xor(readers[j], me)
-            x = q_all[slot]
+            x = q_in[slot // 2, lax.rem(slot, 2)].astype(jnp.float32)
             for g in range(groups):
                 for h in range(group):
                     first = (h * n_readers + j) * rows
@@ -186,29 +193,33 @@
         total = group * n_readers * rows
         blocks = total // block
 
-        for kind, buf in ((0, keys), (1, values)):
+        def arrived(kind, buf):
             pltpu.make_async_copy(mate_kv.at[kind], buf, kv_sems.at[kind]).wait()
+
+        arrived(0, keys)
         for g in range(groups):
-
-            @pl.loop(0, blocks)
-            def _(i):
-                part = pl.ds(pl.multiple_of(i * block, block), block)
-                q = q_rows[g, part, :].astype(jnp.bfloat16)
+            for i in range(blocks):
+                span = slice(i * block, (i + 1) * block)
+                q = q_rows[g, span, :].astype(jnp.bfloat16)
                 k = keys[:, g * HD : (g + 1) * HD]
                 s = lax.dot_general(q, k, (((1,), (1,)), ((), ())), preferred_element_type=jnp.float32)
                 top = jnp.max(s, axis=1, keepdims=True)
                 p = jnp.exp2((s - top) * (scale * LOG2E))
                 den = jnp.sum(p, axis=1, keepdims=True)
+                if g == 0 and i == 0:
+                    arrived(1, values)
                 v = values[:, g * HD : (g + 1) * HD]
                 o = jnp.dot(p.astype(jnp.bfloat16), v, preferred_element_type=jnp.float32)
-                o_rows[g, part, :] = o * (1.0 / den)
-                lse_rows[g, part, :] = jnp.broadcast_to(top * scale + jnp.log(den), (block, 128))
+                o_rows[g, span, :] = o * (1.0 / den)
+                lse_rows[g, span, :] = jnp.broadcast_to(top * scale + jnp.log(den), (block, 128))
 
         lane = lax.broadcasted_iota(jnp.int32, (rows, 128), 1)
         heads = groups * group
+        for slot in range(2 * chips):
+            o_all[slot, :, half:] = jnp.zeros((rows, 128), jnp.float32)
         for j in range(n_readers):
             slot = jnp.bitwise_xor(readers[j], me)
-            stat = jnp.zeros((rows, 128), jnp.float32)
+            stat = jnp.where(lane == 127, 1.0, 0.0)
             for g in range(groups):
                 for h in range(group):
                     first = (h * n_readers + j) * rows
@@ -236,31 +247,40 @@
         out[:, cols] = jnp.dot(attn[...], w[first + j], preferred_element_type=jnp.float32)
 
 
-def away_kernel(heads, plan, readers, near, far, res, res_lse, w_hbm, w, *refs):
+def merge(heads, core, part, res, res_lse, store):
+    stat = part[:, heads * HD :].astype(jnp.float32)
+    is_reader = stat[:, 127:128]
+    pre = stat + pltpu.roll(stat, 128 - heads, 1) + pltpu.roll(stat, 128 - 2 * heads, 1)
+    weights = 1.0 / (1.0 + jnp.exp(res_lse[core] - pre))
+    for h in range(heads):
+        cols = slice(h * HD, (h + 1) * HD)
+        r = res[core, :, cols]
+        y = r + weights[:, h : h + 1] * (part[:, cols].astype(jnp.float32) - r)
+        store(h, jnp.where(is_reader > 0.5, y, r).astype(jnp.bfloat16))
+
+
+def near_kernel(heads, part, res, res_lse, out):
+    def store(h, x):
+        out[:, h * HD : (h + 1) * HD] = x
+
+    merge(heads, lax.rem(place(), 2), part, res, res_lse, store)
+
+
+def away_kernel(heads, plan, near, far, res, res_lse, w_hbm, w, *refs):
     n_tp, chunk, width = plan
     per_chunk = chunk // width
     outs, (attn, w_late, w_sems) = refs[: n_tp - 1], refs[n_tp - 1 :]
     copies = w_copies(plan, n_tp * per_chunk - w_late.shape[0], w_hbm, w_late, w_sems)
     for copy in copies:
         copy.start()
-    me = place()
-    core = lax.rem(me, 2)
-    is_reader = jnp.int32(0)
-    for j in range(readers.shape[0]):
-        is_reader = jnp.where(readers[j] == me, 1, is_reader)
     half = heads * HD
-    for side in range(2):
-        mine = core == side
-        stat = jnp.where(mine, near[:, half:].astype(jnp.float32), far[:, half:].astype(jnp.float32))
-        pre = stat + pltpu.roll(stat, 128 - heads, 1) + pltpu.roll(stat, 128 - 2 * heads, 1)
-        weights = 1.0 / (1.0 + jnp.exp(res_lse[side] - pre))
-        for h in range(heads):
-            weight = weights[:, h : h + 1]
-            cols = slice(h * HD, (h + 1) * HD)
-            r = res[side, :, cols]
-            x = jnp.where(mine, near[:, cols].astype(jnp.float32), far[:, cols].astype(jnp.float32))
-            y = jnp.where(is_reader > 0, r + weight * (x - r), r)
-            attn[:, side * half + h * HD : side * half + (h + 1) * HD] = y.astype(jnp.bfloat16)
+    core = lax.rem(place(), 2)
+    attn[:, pl.ds(pl.multiple_of(core * half, half), half)] = near[...]
+
+    def store(h, x):
+        attn[:, pl.ds(pl.multiple_of((1 - core) * half + h * HD, HD), HD)] = x
+
+    merge(heads, 1 - core, far, res, res_lse, store)
     for i, out in enumerate(outs):
         project(attn, w, i * per_chunk, per_chunk, out, 0)
     for copy in copies:
@@ -295,11 +315,11 @@
     def hop(x, d):
         return lax.ppermute(x, "dp", [(i, i ^ d) for i in range(n_dp)])
 
-    mine, other = pl.pallas_call(
+    mine, other, queries = pl.pallas_call(
         functools.partial(split_kernel, half),
-        out_shape=tuple(jax.ShapeDtypeStruct((rows, half), jnp.bfloat16) for _ in range(2)),
+        out_shape=tuple(jax.ShapeDtypeStruct((rows, n), jnp.bfloat16) for n in (half, half, 2 * half)),
         in_specs=[vmem_spec()],
-        out_specs=(vmem_spec(), vmem_spec()),
+        out_specs=(vmem_spec(),) * 3,
         compiler_params=pltpu.CompilerParams(vmem_limit_bytes=2 << 20),
         name="split",
     )(queries)
@@ -312,7 +332,7 @@
         out_specs=vmem_spec(),
         scratch_shapes=[pltpu.SemaphoreType.DMA(())],
         compiler_params=pltpu.CompilerParams(vmem_limit_bytes=4 << 20),
-        cost_estimate=pl.CostEstimate(flops=1 << 24, bytes_accessed=4 * prefix * kv_cols, transcendentals=0),
+        cost_estimate=pl.CostEstimate(flops=1 << 32, bytes_accessed=1 << 24, transcendentals=0),
         name="share",
     )(in_hbm(prefix_kv), other)
     pair = pl.pallas_call(
@@ -321,12 +341,11 @@
         in_specs=[vmem_spec()] * 3,
         out_specs=vmem_spec(),
         compiler_params=pltpu.CompilerParams(vmem_limit_bytes=2 << 20),
-        cost_estimate=pl.CostEstimate(flops=1 << 32, bytes_accessed=1 << 24, transcendentals=0),
         name="pair",
     )(mine, got, shared)
     width = min(512, chunk)
     plan = (n_tp, chunk, width)
-    last = min(3, chunk // width)
+    last = min(2, chunk // width)
     counts = (d_out // width - last, last)
 
     def w_blocks(n):
@@ -342,7 +361,9 @@
         return lax.ppermute(x, "dp", pairs)
 
     def gather(root, pair, shared, table, lengths, queries, cache_kv):
-        got = [with_chip(pair, root, d) for d in range(1, chips)]
+        got = []
+        for d in range(1, chips):
+            got.append(with_chip(pair, root, d))
         mate_kv = hop(shared, 1)
         res, res_lse = pl.pallas_call(
             functools.partial(resident_kernel, rows, groups, group, maxpages),
@@ -367,7 +388,7 @@
         )(table, lengths, queries, in_hbm(cache_kv))
         return (*got, mate_kv, res, res_lse)
 
-    def finish(root, w_out, owner, readers, res, res_lse, *pre):
+    def finish(root, w_out, owner, res, res_lse, *pre):
         back = [pre[0]] + [with_chip(pre[d], root, d) for d in range(1, chips)]
         loaded, token = pl.pallas_call(
             functools.partial(load_kernel, plan),
@@ -380,14 +401,23 @@
             name="load",
         )(in_hbm(w_out), pre[0])
         near, other = pl.pallas_call(
-            functools.partial(choose_kernel, chips),
+            functools.partial(choose_kernel, chips, root),
             out_shape=tuple(jax.ShapeDtypeStruct((rows, wide), jnp.bfloat16) for _ in range(2)),
-            in_specs=[smem_spec()] + [vmem_spec()] * (chips + 1),
+            in_specs=[vmem_spec()] * (chips + 1) + ([smem_spec()] if root is None else []),
             out_specs=(vmem_spec(), vmem_spec()),
             compiler_params=pltpu.CompilerParams(vmem_limit_bytes=4 << 20),
             name="choose",
-        )(owner, *back, token)
+        )(*back, token, *([owner] if root is None else []))
         far = hop(other, 1)
+        near = pl.pallas_call(
+            functools.partial(near_kernel, half_heads),
+            out_shape=jax.ShapeDtypeStruct((rows, half), jnp.bfloat16),
+            in_specs=[vmem_spec()] * 3,
+            out_specs=vmem_spec(),
+            compiler_params=pltpu.CompilerParams(vmem_limit_bytes=4 << 20),
+            cost_estimate=pl.CostEstimate(flops=1 << 20, bytes_accessed=1 << 17, transcendentals=0),
+            name="near",
+        )(near, res, res_lse)
         in_vmem = functools.partial(pltpu.with_memory_space_constraint, memory_space=VMEM)
         cost = pl.CostEstimate(
             flops=2 * rows * heads * HD * chunk * 16, bytes_accessed=2 * heads * HD * chunk, transcendentals=0
@@ -396,13 +426,13 @@
             functools.partial(away_kernel, half_heads, plan),
             out_shape=tuple(jax.ShapeDtypeStruct((rows, chunk), jnp.float32) for _ in range(n_tp - 1))
             + (jax.ShapeDtypeStruct((rows, heads * HD), jnp.bfloat16), w_blocks(counts[1])),
-            in_specs=[smem_spec()] + [vmem_spec()] * 4 + [hbm_spec(), vmem_spec()],
+            in_specs=[vmem_spec()] * 4 + [hbm_spec(), vmem_spec()],
             out_specs=(vmem_spec(),) * (n_tp + 1),
             scratch_shapes=[pltpu.SemaphoreType.DMA((counts[1],))],
             compiler_params=pltpu.CompilerParams(vmem_limit_bytes=4 << 20),
             cost_estimate=cost,
             name="away",
-        )(readers, near, far, res, res_lse, in_hbm(w_out), in_vmem(loaded))
+        )(near, far, res, res_lse, in_hbm(w_out), in_vmem(loaded))
         home = pl.pallas_call(
             home_kernel,
             out_shape=jax.ShapeDtypeStruct((rows, chunk), jnp.float32),
@@ -419,7 +449,7 @@
     def routed(step, *operands):
         if chips > 8:
             return step(None, *operands)
-        return lax.switch(owner[0] // 2, [functools.partial(step, k) for k in range(chips)], *operands)
+        return lax.switch(lax.shift_right_logical(owner[0], 1), [functools.partial(step, k) for k in range(chips)], *operands)
 
     *gathered, mate_kv, res, res_lse = routed(gather, pair, shared, page_table[0], lengths, queries, cache_kv)
     gathered = [pair] + gathered
@@ -428,17 +458,18 @@
     pre = pl.pallas_call(
         functools.partial(prefix_kernel, chips, rows, half_groups, share_group, n_readers, block),
         out_shape=tuple(jax.ShapeDtypeStruct((2, rows, wide), jnp.bfloat16) for _ in range(chips)),
-        in_specs=[smem_spec(), smem_spec()] + [vmem_spec()] * chips + [hbm_spec()] * 2,
+        in_specs=[smem_spec(), smem_spec()] + [vmem_spec()] + [hbm_spec()] * (chips + 1),
         out_specs=(vmem_spec(),) * chips,
         scratch_shapes=[
             VMEM((prefix, kv_cols), jnp.bfloat16),
             VMEM((prefix, kv_cols), jnp.bfloat16),
-            VMEM((2 * chips, rows, half), jnp.float32),
+            VMEM((chips, 2, rows, half), jnp.bfloat16),
             VMEM((half_groups, total, HD), jnp.float32),
             VMEM((half_groups, total, HD), jnp.float32),
             VMEM((half_groups, total, 128), jnp.float32),
             VMEM((2 * chips, rows, wide), jnp.float32),
             pltpu.SemaphoreType.DMA((2,)),
+            pltpu.SemaphoreType.DMA((chips,)),
         ],
         compiler_params=pltpu.CompilerParams(vmem_limit_bytes=16 << 20),
         cost_estimate=pl.CostEstimate(
@@ -447,8 +478,8 @@
             transcendentals=half_groups * total * prefix,
         ),
         name="prefix",
-    )(owner, readers, *gathered, in_hbm(prefix_kv), in_hbm(mate_kv))
-    return routed(finish, w_out, owner, readers, res, res_lse, *pre)
+    )(owner, readers, gathered[0], *map(in_hbm, gathered[1:]), in_hbm(prefix_kv), in_hbm(mate_kv))
+    return routed(finish, w_out, owner, res, res_lse, *pre)
 
 
 def solution(mesh):

time: 60.9 us -> 56 us (0.920)
  between operations: 2.72 us -> 0.15 us
  Pallas kernels: 26.5 us -> 24.3 us
  local copies, waits for them, and re-layouts: 0.63 us -> 1.47 us
    pallas_call x1, Pallas kernels: 5.28 us -> 3.5 us  [finish(): pl.pallas_call(functools.partial(away_kernel, half_heads, plan), out_shap...]
    pallas_call x1, Pallas kernels: 7.15 us -> 8.37 us  [finish(): pl.pallas_call(functools.partial(load_kernel, plan), out_shape=(w_blocks(...]
    pallas_call x1, Pallas kernels: 0.91 us -> 0.01 us  [shards(): pl.pallas_call(functools.partial(split_kernel, half), out_shape=tuple((ja...]
    unnamed x12, local copies, waits for them, and re-layouts: 0.63 us -> 1.47 us
    ppermute x14, starting transfers between devices: 24.2 us -> 23.5 us  [with_chip(): return lax.ppermute(x, 'dp', pairs)]
  transfers between devices with their start and end apart: 18 -> 18, of which waited for: 3 -> 3; matrix products, arithmetic and copies ran while one was open for 0% -> 0% of each run, Pallas kernels for 31% -> 36%
where the time goes in v3:
time: 56 us; the launch traced here: 55.8 us
  starting transfers between devices  25.8 us (46%)
  Pallas kernels  24.3 us (43%)
  waiting for transfers between devices  3.72 us (7%)
  local copies, waits for them, and re-layouts  1.47 us (3%)
    ppermute x14, starting transfers between devices, with_chip(): return lax.ppermute(x, 'dp', pairs)  23.5 us
    pallas_call x1, Pallas kernels, finish(): pl.pallas_call(functools.partial(load_kernel, plan), out_shape=(w_blocks(...  8.37 us
    pallas_call x1, Pallas kernels, gather(): pl.pallas_call(functools.partial(resident_kernel, rows, groups, group, ma...  7.26 us
    pallas_call x1, Pallas kernels, finish(): pl.pallas_call(functools.partial(away_kernel, half_heads, plan), out_shap...  3.5 us
    pallas_call x1, Pallas kernels, finish(): pl.pallas_call(home_kernel, out_shape=jax.ShapeDtypeStruct((rows, chunk),...  2.61 us
    ppermute x14, waiting for transfers between devices, with_chip(): return lax.ppermute(x, 'dp', pairs)  2.57 us
    pallas_call x1, Pallas kernels, shards(): pl.pallas_call(functools.partial(share_kernel, kv_cols), out_shape=jax.Sh...  1.6 us
    ppermute x1, starting transfers between devices, finish(): lax.ppermute(away[k - 1], 'tp', [(i, i ^ k) for i in range(n_tp)])  1.57 us
  transfers between devices with their start and end apart: 18, of which 3 were waited for; matrix products, arithmetic and copies ran while one was open for 0% of the time, Pallas kernels for 36%

profile of v3, /device:TPU:0, one launch (start us, length us, event | category | flops | bytes accessed | tf_op | source)
XLA Modules:
  0.0 55.8 jit_solution(1287286510979497216)
XLA Ops:
  0.0 0.8 %copy-done = bf16[8,4096]{1,0:T(8,128)(2,1)S(1)} copy-done((bf16[8,4096]{1,0:T(8,128)(2,1)S(1)}, bf16[8,4096]{1,0:T(8,128)(2,1)}, u32[]{:S(2)}) %copy-start) | copy-done | bytes 65560
  0.9 0.6 collective-permute-start.136
  1.4 1.6 %share.1.after = bf16[2,2048,256]{2,1,0:T(8,128)(2,1)S(1)} custom-call(bf16[2,2048,512]{2,1,0:T(8,128)(2,1)} %refs_8_.1, bf16[8,2048]{1,0:T(8,128)(2,1)S(1)} %get-tuple-element.522.after), custom_call_target="tpu_custom_call" | custom-call | flops 4294967296 | bytes 16777216 | tf_op jit(solution)/shard_map/share/pallas_call | solution.py:328
  3.1 17.3 %conditional.4 = (bf16[2,8,2048]{2,1,0:T(8,128)(2,1)}, bf16[2,8,2048]{2,1,0:T(8,128)(2,1)}, bf16[2,8,2048]{2,1,0:T(8,128)(2,1)}, bf16[2,8,2048]{2,1,0:T(8,128)(2...) conditional(s32[]{:T(128)} %bitcast, ...), branch_computations={%region_0.0_spmd, %region_1.0_spmd, %region_2.0_spmd, %region_3.0_... | conditional | flops 536870912 | bytes 18612624 | solution.py:452
  3.3 6.0 %collective-permute-start.62 = (bf16[2,8,2048]{2,1,0:T(8,128)(2,1)S(1)}, bf16[2,8,2048]{2,1,0:T(8,128)(2,1)}, u32[]{:S(2)}, u32[]{:S(2)}) collective-permute-start(bf16[2,8,2048]{2,1,0:T(8,128)(2,1)S(1)} %get-tuple-element.348), channel_id=1, source_target_pairs={{0,28},{2,30},{4,6},{6,4},{8,10},{10,8},{12,14},{14,12},{16,18},{1... | collective-permute-start | bytes 196616 | tf_op jit(solution)/shard_map/cond/branch_7_fun/ppermute | solution.py:361
  9.3 0.5 collective-permute-start.60
  9.8 2.5 %collective-permute-done.62 = bf16[2,8,2048]{2,1,0:T(8,128)(2,1)} collective-permute-done((bf16[2,8,2048]{2,1,0:T(8,128)(2,1)S(1)}, bf16[2,8,2048]{2,1,0:T(8,128)(2,1)}, u32[]{:S(2)}, u32[]{:S(2)}) %collective-permute-start.62) | collective-permute-done | bytes 65568 | tf_op jit(solution)/shard_map/cond/branch_7_fun/ppermute | solution.py:361
  12.3 0.5 collective-permute-start.57
  12.9 7.3 %resident.15 = (f32[2,8,2048]{2,1,0:T(8,128)S(1)}, f32[2,8,128]{2,1,0:T(8,128)S(1)}) custom-call(s32[64]{0:T(128)S(1)} %get-tuple-element.350.table, s32[8]{0:T(128)S(1)} %get-tuple-element.351.lengths, bf16[8,4096]{1,0:T(8,128)(2,1)S(1)} %get-tuple-element.352.q_ref, bf16[2,64,64,512]{3,2,1,0:T(8,128)(2,1)} %get-tuple-element.353.cache), custom_call_target="tpu_custom_call" | custom-call | flops 536870912 | bytes 8388608 | tf_op jit(solution)/shard_map/cond/branch_7_fun/resident/pallas_call | solution.py:368
  20.4 0.7 %prefix.1 = (bf16[2,8,2176]{2,1,0:T(8,128)(2,1)S(1)}, bf16[2,8,2176]{2,1,0:T(8,128)(2,1)S(1)}, bf16[2,8,2176]{2,1,0:T(8,128)(2,1)S(1)}, bf16[2,8,2176]{2,1,0:T(8...) custom-call(s32[16]{0:T(128)S(1)} %copy-done.1, ...), custom_call_target="tpu_custom_call" | custom-call | flops 1073741824 | bytes 2097152 | tf_op jit(solution)/shard_map/prefix/pallas_call | solution.py:458
  21.1 34.1 %conditional.6 = (bf16[8,2048]{1,0:T(8,128)(2,1)S(1)}) conditional(s32[]{:T(128)} %bitcast, (bf16[2,8,2176]{2,1,0:T(8,128)(2,1)S(1)}, bf16[2,8,2176]{2,1,0:T(8,128)(2,1)S(1)}, bf16[2,8,2176]{2,1,0:T(8,128)(2,1)S(1)}, bf16[2,8,2176]{2,1,0:T(8,128)(2,1)S(1)}, bf16[2,8,2176]{2,1,0:T(8,128)(2,1)S(1)}, ...), branch_computations={%region_8.0_spmd, %region_9.0_spmd, %region_10.0_spmd, %region_11.... | conditional | flops 4564467712 | bytes 52978032
  21.2 0.5 collective-permute-start.127
  21.7 0.4 collective-permute-start.129
  22.2 0.4 collective-permute-start.131
  22.7 0.2 collective-permute-start.132
  22.9 14.6 %collective-permute-start.133 = (bf16[2,8,2176]{2,1,0:T(8,128)(2,1)S(1)}, bf16[2,8,2176]{2,1,0:T(8,128)(2,1)S(1)}, u32[]{:S(2)}, u32[]{:S(2)}) collective-permute-start(bf16[2,8,2176]{2,1,0:T(8,128)(2,1)S(1)} %get-tuple-element.489), channel_id=1, source_target_pairs={{0,28},{2,30},{4,6},{6,4},{8,10},{10,8},{12,14},{14,12},{16,18},{1... | collective-permute-start | bytes 208904 | tf_op jit(solution)/shard_map/cond/branch_7_fun/ppermute | solution.py:361
  37.5 8.4 %load.15 = (bf16[6,4096,512]{2,1,0:T(8,128)(2,1)S(1)}, f32[8,128]{1,0:T(8,128)S(1)}) custom-call(bf16[4096,4096]{1,0:T(8,128)(2,1)} %get-tuple-element.490.w.w_hbm, bf16[2,8,2176]{2,1,0:T(8,128)(2,1)S(1)} %get-tuple-element.482.after.refs_0_), custom_call_target="tpu_custom_call" | custom-call | flops 268435456 | bytes 16777216 | tf_op jit(solution)/shard_map/cond/branch_7_fun/load/pallas_call | solution.py:393
  46.1 0.2 near.15
  46.3 1.0 %collective-permute-done.134.far = bf16[8,2176]{1,0:T(8,128)(2,1)S(1)} collective-permute-done((bf16[8,2176]{1,0:T(8,128)(2,1)S(1)}, bf16[8,2176]{1,0:T(8,128)(2,1)S(1)}, u32[]{:S(2)}, u32[]{:S(2)}) %collective-permute-start.134) | collective-permute-done | bytes 34848 | tf_op jit(solution)/shard_map/cond/branch_7_fun/ppermute | solution.py:316
  47.3 3.5 %away.15 = (f32[8,2048]{1,0:T(8,128)S(1)}, bf16[8,4096]{1,0:T(8,128)(2,1)S(1)}, bf16[2,4096,512]{2,1,0:T(8,128)(2,1)S(1)}) custom-call(bf16[8,2048]{1,0:T(8,128)(2,1)S(1)} %near.15, bf16[8,2176]{1,0:T(8,128)(2,1)S(1)} %collective-permute-done.134.far, f32[2,8,2048]{2,1,0:T(8,128)S(1)} %get-tuple-element.493.res, ...), custom_call_target="tpu_custom_call" | custom-call | flops 2147483648 | bytes 16777216 | tf_op jit(solution)/shard_map/cond/branch_7_fun/away/pallas_call | solution.py:425
  50.8 1.6 %collective-permute-start.135 = (f32[8,2048]{1,0:T(8,128)S(1)}, f32[8,2048]{1,0:T(8,128)S(1)}, u32[]{:S(2)}, u32[]{:S(2)}) collective-permute-start(f32[8,2048]{1,0:T(8,128)S(1)} %get-tuple-element.499), channel_id=1, source_target_pairs={{0,1},{1,0},{2,3},{3,2},{4,5},{5,4},{6,7},{7,6},{8,9},{9,8},{10,11... | collective-permute-start | bytes 196616 | tf_op jit(solution)/shard_map/cond/branch_7_fun/ppermute | solution.py:446
  52.4 2.6 %home.15 = f32[8,2048]{1,0:T(8,128)S(1)} custom-call(bf16[8,4096]{1,0:T(8,128)(2,1)S(1)} %get-tuple-element.497.attn, bf16[6,4096,512]{2,1,0:T(8,128)(2,1)S(1)} %get-tuple-element.496.w, bf16[2,4096,512]{2,1,0:T(8,128)(2,1)S(1)} %get-tuple-element.498.w_late), custom_call_target="tpu_custom_call" | custom-call | flops 2147483648 | bytes 16777216 | tf_op jit(solution)/shard_map/cond/branch_7_fun/home/pallas_call | solution.py:436
  55.0 0.1 collective-permute-done.135
  55.2 0.6 %copy-done.5 = bf16[8,2048]{1,0:T(8,128)(2,1)} copy-done((bf16[8,2048]{1,0:T(8,128)(2,1)}, bf16[8,2048]{1,0:T(8,128)(2,1)S(1)}, u32[]{:S(2)}) %copy-start.5) | copy-done | bytes 32792
  (37 shorter events, 0.6 us)
Async XLA Ops:
  0.0 0.8 %copy-start = (bf16[8,4096]{1,0:T(8,128)(2,1)S(1)}, bf16[8,4096]{1,0:T(8,128)(2,1)}, u32[]{:S(2)}) copy-start(bf16[8,4096]{1,0:T(8,128)(2,1)} %q_ref.1) | copy-start | bytes 196612
  0.8 2.2 %copy-start.1 = (s32[16]{0:T(128)S(1)}, s32[16]{0:T(128)}, u32[]{:S(2)}) copy-start(s32[16]{0:T(128)} %owner_ref.1) | copy-start | bytes 196
  0.9 2.3 %copy-start.3 = (s32[1,64]{1,0:T(1,128)S(1)}, s32[1,64]{1,0:T(1,128)}, u32[]{:S(2)}) copy-start(s32[1,64]{1,0:T(1,128)} %param.28) | copy-start | bytes 772
  0.9 2.3 %copy-start.4 = (s32[8]{0:T(128)S(1)}, s32[8]{0:T(128)}, u32[]{:S(2)}) copy-start(s32[8]{0:T(128)} %param.27) | copy-start | bytes 100
  0.9 2.2 %collective-permute-start.136 = (bf16[8,2048]{1,0:T(8,128)(2,1)S(1)}, bf16[8,2048]{1,0:T(8,128)(2,1)S(1)}, u32[]{:S(2)}, u32[]{:S(2)}) collective-permute-start(bf16[8,2048]{1,0:T(8,128)(2,1)S(1)} %get-tuple-element.522.after), channel_id=1, source_target_pairs={{0,2},{2,0},{4,6},{6,4},{8,10},{10,8},{12,14},{14,12},{16,18},{18,... | collective-permute-start | bytes 98312 | tf_op jit(solution)/shard_map/ppermute | solution.py:316
  3.1 17.3 %copy-start.2 = (s32[8]{0:T(128)S(1)}, s32[8]{0:T(128)}, u32[]{:S(2)}) copy-start(s32[8]{0:T(128)} %readers.1) | copy-start | bytes 100
  3.2 17.0 %collective-permute-start.63 = (bf16[2,2048,256]{2,1,0:T(8,128)(2,1)S(1)}, bf16[2,2048,256]{2,1,0:T(8,128)(2,1)}, u32[]{:S(2)}, u32[]{:S(2)}) collective-permute-start(bf16[2,2048,256]{2,1,0:T(8,128)(2,1)S(1)} %get-tuple-element.349), channel_id=1, source_target_pairs={{0,2},{2,0},{4,6},{6,4},{8,10},{10,8},{12,14},{14,12},{16,18},{18,... | collective-permute-start | bytes 6291464 | tf_op jit(solution)/shard_map/cond/branch_7_fun/ppermute | solution.py:316
  3.3 9.0 %collective-permute-start.62 = (bf16[2,8,2048]{2,1,0:T(8,128)(2,1)S(1)}, bf16[2,8,2048]{2,1,0:T(8,128)(2,1)}, u32[]{:S(2)}, u32[]{:S(2)}) collective-permute-start(bf16[2,8,2048]{2,1,0:T(8,128)(2,1)S(1)} %get-tuple-element.348), channel_id=1, source_target_pairs={{0,28},{2,30},{4,6},{6,4},{8,10},{10,8},{12,14},{14,12},{16,18},{1... | collective-permute-start | bytes 196616 | tf_op jit(solution)/shard_map/cond/branch_7_fun/ppermute | solution.py:361
  9.3 3.1 %collective-permute-start.61 = (bf16[2,8,2048]{2,1,0:T(8,128)(2,1)S(1)}, bf16[2,8,2048]{2,1,0:T(8,128)(2,1)}, u32[]{:S(2)}, u32[]{:S(2)}) collective-permute-start(bf16[2,8,2048]{2,1,0:T(8,128)(2,1)S(1)} %get-tuple-element.348), channel_id=1, source_target_pairs={{0,2},{2,0},{4,28},{6,30},{8,10},{10,8},{12,14},{14,12},{16,18},{1... | collective-permute-start | bytes 196616 | tf_op jit(solution)/shard_map/cond/branch_7_fun/ppermute | solution.py:361
  9.3 3.6 %collective-permute-start.60 = (bf16[2,8,2048]{2,1,0:T(8,128)(2,1)S(1)}, bf16[2,8,2048]{2,1,0:T(8,128)(2,1)}, u32[]{:S(2)}, u32[]{:S(2)}) collective-permute-start(bf16[2,8,2048]{2,1,0:T(8,128)(2,1)S(1)} %get-tuple-element.348), channel_id=1, source_target_pairs={{0,2},{2,0},{4,6},{6,4},{8,28},{10,30},{12,14},{14,12},{16,18},{18... | collective-permute-start | bytes 196616 | tf_op jit(solution)/shard_map/cond/branch_7_fun/ppermute | solution.py:361
  9.8 10.4 %collective-permute-start.59 = (bf16[2,8,2048]{2,1,0:T(8,128)(2,1)S(1)}, bf16[2,8,2048]{2,1,0:T(8,128)(2,1)}, u32[]{:S(2)}, u32[]{:S(2)}) collective-permute-start(bf16[2,8,2048]{2,1,0:T(8,128)(2,1)S(1)} %get-tuple-element.348), channel_id=1, source_target_pairs={{0,2},{2,0},{4,6},{6,4},{8,10},{10,8},{12,28},{14,30},{16,18},{18,... | collective-permute-start | bytes 196616 | tf_op jit(solution)/shard_map/cond/branch_7_fun/ppermute | solution.py:361
  12.3 7.9 %collective-permute-start.58 = (bf16[2,8,2048]{2,1,0:T(8,128)(2,1)S(1)}, bf16[2,8,2048]{2,1,0:T(8,128)(2,1)}, u32[]{:S(2)}, u32[]{:S(2)}) collective-permute-start(bf16[2,8,2048]{2,1,0:T(8,128)(2,1)S(1)} %get-tuple-element.348), channel_id=1, source_target_pairs={{0,2},{2,0},{4,6},{6,4},{8,10},{10,8},{12,14},{14,12},{16,28},{18,... | collective-permute-start | bytes 196616 | tf_op jit(solution)/shard_map/cond/branch_7_fun/ppermute | solution.py:361
  12.3 7.9 %collective-permute-start.57 = (bf16[2,8,2048]{2,1,0:T(8,128)(2,1)S(1)}, bf16[2,8,2048]{2,1,0:T(8,128)(2,1)}, u32[]{:S(2)}, u32[]{:S(2)}) collective-permute-start(bf16[2,8,2048]{2,1,0:T(8,128)(2,1)S(1)} %get-tuple-element.348), channel_id=1, source_target_pairs={{0,2},{2,0},{4,6},{6,4},{8,10},{10,8},{12,14},{14,12},{16,18},{18,... | collective-permute-start | bytes 196616 | tf_op jit(solution)/shard_map/cond/branch_7_fun/ppermute | solution.py:361
  12.8 7.4 %collective-permute-start.56 = (bf16[2,8,2048]{2,1,0:T(8,128)(2,1)S(1)}, bf16[2,8,2048]{2,1,0:T(8,128)(2,1)}, u32[]{:S(2)}, u32[]{:S(2)}) collective-permute-start(bf16[2,8,2048]{2,1,0:T(8,128)(2,1)S(1)} %get-tuple-element.348), channel_id=1, source_target_pairs={{0,2},{2,0},{4,6},{6,4},{8,10},{10,8},{12,14},{14,12},{16,18},{18,... | collective-permute-start | bytes 196616 | tf_op jit(solution)/shard_map/cond/branch_7_fun/ppermute | solution.py:361
  21.2 1.5 %collective-permute-start.127 = (bf16[2,8,2176]{2,1,0:T(8,128)(2,1)S(1)}, bf16[2,8,2176]{2,1,0:T(8,128)(2,1)S(1)}, u32[]{:S(2)}, u32[]{:S(2)}) collective-permute-start(bf16[2,8,2176]{2,1,0:T(8,128)(2,1)S(1)} %get-tuple-element.483), channel_id=1, source_target_pairs={{0,2},{2,0},{4,6},{6,4},{8,10},{10,8},{12,14},{14,12},{16,18},{18,... | collective-permute-start | bytes 208904 | tf_op jit(solution)/shard_map/cond/branch_7_fun/ppermute | solution.py:361
  21.7 1.3 %collective-permute-start.128 = (bf16[2,8,2176]{2,1,0:T(8,128)(2,1)S(1)}, bf16[2,8,2176]{2,1,0:T(8,128)(2,1)S(1)}, u32[]{:S(2)}, u32[]{:S(2)}) collective-permute-start(bf16[2,8,2176]{2,1,0:T(8,128)(2,1)S(1)} %get-tuple-element.484), channel_id=1, source_target_pairs={{0,2},{2,0},{4,6},{6,4},{8,10},{10,8},{12,14},{14,12},{16,18},{18,... | collective-permute-start | bytes 208904 | tf_op jit(solution)/shard_map/cond/branch_7_fun/ppermute | solution.py:361
  21.7 24.2 %collective-permute-start.129 = (bf16[2,8,2176]{2,1,0:T(8,128)(2,1)S(1)}, bf16[2,8,2176]{2,1,0:T(8,128)(2,1)S(1)}, u32[]{:S(2)}, u32[]{:S(2)}) collective-permute-start(bf16[2,8,2176]{2,1,0:T(8,128)(2,1)S(1)} %get-tuple-element.485), channel_id=1, source_target_pairs={{0,2},{2,0},{4,6},{6,4},{8,10},{10,8},{12,14},{14,12},{16,28},{18,... | collective-permute-start | bytes 208904 | tf_op jit(solution)/shard_map/cond/branch_7_fun/ppermute | solution.py:361
  22.2 23.8 %collective-permute-start.130 = (bf16[2,8,2176]{2,1,0:T(8,128)(2,1)S(1)}, bf16[2,8,2176]{2,1,0:T(8,128)(2,1)S(1)}, u32[]{:S(2)}, u32[]{:S(2)}) collective-permute-start(bf16[2,8,2176]{2,1,0:T(8,128)(2,1)S(1)} %get-tuple-element.486), channel_id=1, source_target_pairs={{0,2},{2,0},{4,6},{6,4},{8,10},{10,8},{12,28},{14,30},{16,18},{18,... | collective-permute-start | bytes 208904 | tf_op jit(solution)/shard_map/cond/branch_7_fun/ppermute | solution.py:361
  22.2 23.7 %collective-permute-start.131 = (bf16[2,8,2176]{2,1,0:T(8,128)(2,1)S(1)}, bf16[2,8,2176]{2,1,0:T(8,128)(2,1)S(1)}, u32[]{:S(2)}, u32[]{:S(2)}) collective-permute-start(bf16[2,8,2176]{2,1,0:T(8,128)(2,1)S(1)} %get-tuple-element.487), channel_id=1, source_target_pairs={{0,2},{2,0},{4,6},{6,4},{8,28},{10,30},{12,14},{14,12},{16,18},{18... | collective-permute-start | bytes 208904 | tf_op jit(solution)/shard_map/cond/branch_7_fun/ppermute | solution.py:361
  22.7 23.3 %collective-permute-start.132 = (bf16[2,8,2176]{2,1,0:T(8,128)(2,1)S(1)}, bf16[2,8,2176]{2,1,0:T(8,128)(2,1)S(1)}, u32[]{:S(2)}, u32[]{:S(2)}) collective-permute-start(bf16[2,8,2176]{2,1,0:T(8,128)(2,1)S(1)} %get-tuple-element.488), channel_id=1, source_target_pairs={{0,2},{2,0},{4,28},{6,30},{8,10},{10,8},{12,14},{14,12},{16,18},{1... | collective-permute-start | bytes 208904 | tf_op jit(solution)/shard_map/cond/branch_7_fun/ppermute | solution.py:361
  22.9 23.0 %collective-permute-start.133 = (bf16[2,8,2176]{2,1,0:T(8,128)(2,1)S(1)}, bf16[2,8,2176]{2,1,0:T(8,128)(2,1)S(1)}, u32[]{:S(2)}, u32[]{:S(2)}) collective-permute-start(bf16[2,8,2176]{2,1,0:T(8,128)(2,1)S(1)} %get-tuple-element.489), channel_id=1, source_target_pairs={{0,28},{2,30},{4,6},{6,4},{8,10},{10,8},{12,14},{14,12},{16,18},{1... | collective-permute-start | bytes 208904 | tf_op jit(solution)/shard_map/cond/branch_7_fun/ppermute | solution.py:361
  46.0 1.3 %collective-permute-start.134 = (bf16[8,2176]{1,0:T(8,128)(2,1)S(1)}, bf16[8,2176]{1,0:T(8,128)(2,1)S(1)}, u32[]{:S(2)}, u32[]{:S(2)}) collective-permute-start(bf16[8,2176]{1,0:T(8,128)(2,1)S(1)} %get-tuple-element.495), channel_id=1, source_target_pairs={{0,2},{2,0},{4,6},{6,4},{8,10},{10,8},{12,14},{14,12},{16,18},{18,... | collective-permute-start | bytes 104456 | tf_op jit(solution)/shard_map/cond/branch_7_fun/ppermute | solution.py:316
  50.8 4.3 %collective-permute-start.135 = (f32[8,2048]{1,0:T(8,128)S(1)}, f32[8,2048]{1,0:T(8,128)S(1)}, u32[]{:S(2)}, u32[]{:S(2)}) collective-permute-start(f32[8,2048]{1,0:T(8,128)S(1)} %get-tuple-element.499), channel_id=1, source_target_pairs={{0,1},{1,0},{2,3},{3,2},{4,5},{5,4},{6,7},{7,6},{8,9},{9,8},{10,11... | collective-permute-start | bytes 196616 | tf_op jit(solution)/shard_map/cond/branch_7_fun/ppermute | solution.py:446
  55.2 0.6 %copy-start.5 = (bf16[8,2048]{1,0:T(8,128)(2,1)}, bf16[8,2048]{1,0:T(8,128)(2,1)S(1)}, u32[]{:S(2)}) copy-start(bf16[8,2048]{1,0:T(8,128)(2,1)S(1)} %get-tuple-element.787) | copy-start | bytes 98308

commit v4 on v3

--- a/solution.py
+++ b/solution.py
@@ -10,6 +10,7 @@
 
 HD = 128
 PAGE = 64
+PIECES = 4
 LOG2E = 1.4426950408889634
 VMEM = pltpu.VMEM
 SMEM = pltpu.SMEM
@@ -47,11 +48,22 @@
     out[1] = got[...]
 
 
-def share_kernel(cols, kv, after, out, sem):
+def piece(length, i):
+    return pl.ds(i * (length // PIECES), length // PIECES)
+
+
+def share_kernel(cols, kv, after, out, sems):
     side = 1 - lax.rem(place(), 2) if kv.shape[2] > cols else 0
-    copy = pltpu.make_async_copy(kv.at[:, :, pl.ds(pl.multiple_of(side * cols, 128), cols)], out, sem)
-    copy.start()
-    copy.wait()
+    columns = pl.ds(pl.multiple_of(side * cols, 128), cols)
+    copies = []
+    for kind in range(2):
+        for i in range(PIECES):
+            span = piece(kv.shape[1], i)
+            source, target = kv.at[kind, span, columns], out.at[kind, span]
+            copies.append(pltpu.make_async_copy(source, target, sems.at[kind * PIECES + i]))
+            copies[-1].start()
+    for copy in copies:
+        copy.wait()
 
 
 def w_copies(plan, first, w, outs, sems):
@@ -270,7 +282,7 @@
     n_tp, chunk, width = plan
     per_chunk = chunk // width
     outs, (attn, w_late, w_sems) = refs[: n_tp - 1], refs[n_tp - 1 :]
-    copies = w_copies(plan, n_tp * per_chunk - w_late.shape[0], w_hbm, w_late, w_sems)
+    copies = w_copies(plan, w.shape[0], w_hbm, w_late, w_sems)
     for copy in copies:
         copy.start()
     half = heads * HD
@@ -287,12 +299,20 @@
         copy.wait()
 
 
-def home_kernel(attn, w, w_late, out):
-    late = w_late.shape[0]
-    early = out.shape[1] // w.shape[2] - late
+def home_kernel(plan, attn, w, w_late, w_hbm, out, w_last, w_sems):
+    n_tp, chunk, width = plan
+    late, last = w_late.shape[0], w_last.shape[0]
+    copies = w_copies(plan, n_tp * (chunk // width) - last, w_hbm, w_last, w_sems)
+    for copy in copies:
+        copy.start()
+    early = max(chunk // width - late - last, 0)
     if early:
         project(attn, w, w.shape[0] - early, early, out, 0)
-    project(attn, w_late, 0, late, out, early * w.shape[2])
+    if chunk // width > last:
+        project(attn, w_late, 0, late, out, early * width)
+    for copy in copies:
+        copy.wait()
+    project(attn, w_last, 0, last, out, chunk - last * width)
 
 
 def shards(n_dp, n_tp, queries, prefix_kv, cache_kv, lengths, page_table, owner, readers, w_out):
@@ -330,7 +350,7 @@
         out_shape=jax.ShapeDtypeStruct((2, prefix, kv_cols), jnp.bfloat16),
         in_specs=[hbm_spec(), vmem_spec()],
         out_specs=vmem_spec(),
-        scratch_shapes=[pltpu.SemaphoreType.DMA(())],
+        scratch_shapes=[pltpu.SemaphoreType.DMA((2 * PIECES,))],
         compiler_params=pltpu.CompilerParams(vmem_limit_bytes=4 << 20),
         cost_estimate=pl.CostEstimate(flops=1 << 32, bytes_accessed=1 << 24, transcendentals=0),
         name="share",
@@ -345,8 +365,8 @@
     )(mine, got, shared)
     width = min(512, chunk)
     plan = (n_tp, chunk, width)
-    last = min(2, chunk // width)
-    counts = (d_out // width - last, last)
+    blocks = d_out // width
+    counts = (blocks - 2, 1, 1) if chunk // width > 2 else (blocks - 1, 1, 1)
 
     def w_blocks(n):
         return VMEM((n, w_out.shape[0], width), w_out.dtype)
@@ -434,14 +454,18 @@
             name="away",
         )(near, far, res, res_lse, in_hbm(w_out), in_vmem(loaded))
         home = pl.pallas_call(
-            home_kernel,
+            functools.partial(home_kernel, plan),
             out_shape=jax.ShapeDtypeStruct((rows, chunk), jnp.float32),
-            in_specs=[vmem_spec()] * 3,
+            in_specs=[vmem_spec()] * 3 + [hbm_spec()],
             out_specs=vmem_spec(),
-            compiler_params=pltpu.CompilerParams(vmem_limit_bytes=4 << 20),
+            scratch_shapes=[
+                VMEM((counts[2], w_out.shape[0], width), w_out.dtype),
+                pltpu.SemaphoreType.DMA((counts[2],)),
+            ],
+            compiler_params=pltpu.CompilerParams(vmem_limit_bytes=8 << 20),
             cost_estimate=cost,
             name="home",
-        )(attn, in_vmem(loaded), in_vmem(late))
+        )(attn, in_vmem(loaded), in_vmem(late), in_hbm(w_out))
         for k in range(1, n_tp):
             home = home + lax.ppermute(away[k - 1], "tp", [(i, i ^ k) for i in range(n_tp)])
         return home.astype(jnp.bfloat16)

time: 56 us -> 55.7 us (level)
    pallas_call x1, Pallas kernels: 3.5 us -> 2.82 us  [finish(): pl.pallas_call(functools.partial(away_kernel, half_heads, plan), out_shap...]
  transfers between devices with their start and end apart: 18 -> 18, of which waited for: 3 -> 2; matrix products, arithmetic and copies ran while one was open for 0% -> 0% of each run, Pallas kernels for 36% -> 37%
where the time goes in v4:
time: 55.7 us; the launch traced here: 55.4 us
  starting transfers between devices  25.8 us (46%)
  Pallas kernels  23.8 us (43%)
  waiting for transfers between devices  3.58 us (6%)
  local copies, waits for them, and re-layouts  1.47 us (3%)
  loops' own time  0.64 us (1%)
    ppermute x14, starting transfers between devices, with_chip(): return lax.ppermute(x, 'dp', pairs)  23.5 us
    pallas_call x1, Pallas kernels, finish(): pl.pallas_call(functools.partial(load_kernel, plan), out_shape=(w_blocks(...  8.37 us
    pallas_call x1, Pallas kernels, gather(): pl.pallas_call(functools.partial(resident_kernel, rows, groups, group, ma...  7.26 us
    pallas_call x1, Pallas kernels, finish(): pl.pallas_call(functools.partial(home_kernel, plan), out_shape=jax.ShapeD...  2.85 us
    pallas_call x1, Pallas kernels, finish(): pl.pallas_call(functools.partial(away_kernel, half_heads, plan), out_shap...  2.82 us
    ppermute x14, waiting for transfers between devices, with_chip(): return lax.ppermute(x, 'dp', pairs)  2.57 us
    ppermute x1, starting transfers between devices, finish(): lax.ppermute(away[k - 1], 'tp', [(i, i ^ k) for i in range(n_tp)])  1.59 us
    pallas_call x1, Pallas kernels, shards(): pl.pallas_call(functools.partial(share_kernel, kv_cols), out_shape=jax.Sh...  1.57 us
  transfers between devices with their start and end apart: 18, of which 2 were waited for; matrix products, arithmetic and copies ran while one was open for 0% of the time, Pallas kernels for 37%

profile of v4, /device:TPU:0, one launch (start us, length us, event | category | flops | bytes accessed | tf_op | source)
XLA Modules:
  0.0 55.4 jit_solution(8704268633601040763)
XLA Ops:
  0.0 0.8 %copy-done = bf16[8,4096]{1,0:T(8,128)(2,1)S(1)} copy-done((bf16[8,4096]{1,0:T(8,128)(2,1)S(1)}, bf16[8,4096]{1,0:T(8,128)(2,1)}, u32[]{:S(2)}) %copy-start) | copy-done | bytes 65560
  0.9 0.6 %collective-permute-start.136 = (bf16[8,2048]{1,0:T(8,128)(2,1)S(1)}, bf16[8,2048]{1,0:T(8,128)(2,1)S(1)}, u32[]{:S(2)}, u32[]{:S(2)}) collective-permute-start(bf16[8,2048]{1,0:T(8,128)(2,1)S(1)} %get-tuple-element.522.after), channel_id=1, source_target_pairs={{0,2},{2,0},{4,6},{6,4},{8,10},{10,8},{12,14},{14,12},{16,18},{18,... | collective-permute-start | bytes 98312 | tf_op jit(solution)/shard_map/ppermute | solution.py:336
  1.4 1.6 %share.1.after = bf16[2,2048,256]{2,1,0:T(8,128)(2,1)S(1)} custom-call(bf16[2,2048,512]{2,1,0:T(8,128)(2,1)} %refs_8_.1, bf16[8,2048]{1,0:T(8,128)(2,1)S(1)} %get-tuple-element.522.after), custom_call_target="tpu_custom_call" | custom-call | flops 4294967296 | bytes 16777216 | tf_op jit(solution)/shard_map/share/pallas_call | solution.py:348
  3.1 17.3 %conditional.4 = (bf16[2,8,2048]{2,1,0:T(8,128)(2,1)}, bf16[2,8,2048]{2,1,0:T(8,128)(2,1)}, bf16[2,8,2048]{2,1,0:T(8,128)(2,1)}, bf16[2,8,2048]{2,1,0:T(8,128)(2...) conditional(s32[]{:T(128)} %bitcast, ...), branch_computations={%region_0.0_spmd, %region_1.0_spmd, %region_2.0_spmd, %region_3.0_... | conditional | flops 536870912 | bytes 18612624 | solution.py:476
  3.2 0.1 collective-permute-start.63
  3.3 6.0 %collective-permute-start.62 = (bf16[2,8,2048]{2,1,0:T(8,128)(2,1)S(1)}, bf16[2,8,2048]{2,1,0:T(8,128)(2,1)}, u32[]{:S(2)}, u32[]{:S(2)}) collective-permute-start(bf16[2,8,2048]{2,1,0:T(8,128)(2,1)S(1)} %get-tuple-element.348), channel_id=1, source_target_pairs={{0,28},{2,30},{4,6},{6,4},{8,10},{10,8},{12,14},{14,12},{16,18},{1... | collective-permute-start | bytes 196616 | tf_op jit(solution)/shard_map/cond/branch_7_fun/ppermute | solution.py:381
  9.3 0.5 collective-permute-start.60
  9.8 2.5 %collective-permute-done.62 = bf16[2,8,2048]{2,1,0:T(8,128)(2,1)} collective-permute-done((bf16[2,8,2048]{2,1,0:T(8,128)(2,1)S(1)}, bf16[2,8,2048]{2,1,0:T(8,128)(2,1)}, u32[]{:S(2)}, u32[]{:S(2)}) %collective-permute-start.62) | collective-permute-done | bytes 65568 | tf_op jit(solution)/shard_map/cond/branch_7_fun/ppermute | solution.py:381
  12.3 0.5 collective-permute-start.57
  12.9 7.3 %resident.15 = (f32[2,8,2048]{2,1,0:T(8,128)S(1)}, f32[2,8,128]{2,1,0:T(8,128)S(1)}) custom-call(s32[64]{0:T(128)S(1)} %get-tuple-element.350.table, s32[8]{0:T(128)S(1)} %get-tuple-element.351.lengths, bf16[8,4096]{1,0:T(8,128)(2,1)S(1)} %get-tuple-element.352.q_ref, bf16[2,64,64,512]{3,2,1,0:T(8,128)(2,1)} %get-tuple-element.353.cache), custom_call_target="tpu_custom_call" | custom-call | flops 536870912 | bytes 8388608 | tf_op jit(solution)/shard_map/cond/branch_7_fun/resident/pallas_call | solution.py:388
  20.4 0.7 %prefix.1 = (bf16[2,8,2176]{2,1,0:T(8,128)(2,1)S(1)}, bf16[2,8,2176]{2,1,0:T(8,128)(2,1)S(1)}, bf16[2,8,2176]{2,1,0:T(8,128)(2,1)S(1)}, bf16[2,8,2176]{2,1,0:T(8...) custom-call(s32[16]{0:T(128)S(1)} %copy-done.1, ...), custom_call_target="tpu_custom_call" | custom-call | flops 1073741824 | bytes 2097152 | tf_op jit(solution)/shard_map/prefix/pallas_call | solution.py:482
  21.1 33.7 %conditional.6 = (bf16[8,2048]{1,0:T(8,128)(2,1)S(1)}) conditional(s32[]{:T(128)} %bitcast, (bf16[2,8,2176]{2,1,0:T(8,128)(2,1)S(1)}, bf16[2,8,2176]{2,1,0:T(8,128)(2,1)S(1)}, bf16[2,8,2176]{2,1,0:T(8,128)(2,1)S(1)}, bf16[2,8,2176]{2,1,0:T(8,128)(2,1)S(1)}, bf16[2,8,2176]{2,1,0:T(8,128)(2,1)S(1)}, ...), branch_computations={%region_8.0_spmd, %region_9.0_spmd, %region_10.0_spmd, %region_11.... | conditional | flops 4564467712 | bytes 52978032
  21.4 0.5 collective-permute-start.127
  21.9 0.4 collective-permute-start.129
  22.5 0.4 collective-permute-start.131
  22.9 0.2 collective-permute-start.132
  23.1 14.6 %collective-permute-start.133 = (bf16[2,8,2176]{2,1,0:T(8,128)(2,1)S(1)}, bf16[2,8,2176]{2,1,0:T(8,128)(2,1)S(1)}, u32[]{:S(2)}, u32[]{:S(2)}) collective-permute-start(bf16[2,8,2176]{2,1,0:T(8,128)(2,1)S(1)} %get-tuple-element.489), channel_id=1, source_target_pairs={{0,28},{2,30},{4,6},{6,4},{8,10},{10,8},{12,14},{14,12},{16,18},{1... | collective-permute-start | bytes 208904 | tf_op jit(solution)/shard_map/cond/branch_7_fun/ppermute | solution.py:381
  37.7 8.4 %load.15 = (bf16[6,4096,512]{2,1,0:T(8,128)(2,1)S(1)}, f32[8,128]{1,0:T(8,128)S(1)}) custom-call(bf16[4096,4096]{1,0:T(8,128)(2,1)} %get-tuple-element.490.w.w_hbm, bf16[2,8,2176]{2,1,0:T(8,128)(2,1)S(1)} %get-tuple-element.482.after.refs_0_), custom_call_target="tpu_custom_call" | custom-call | flops 268435456 | bytes 16777216 | tf_op jit(solution)/shard_map/cond/branch_7_fun/load/pallas_call | solution.py:413
  46.3 0.2 near.15
  46.5 1.0 %collective-permute-done.134.far = bf16[8,2176]{1,0:T(8,128)(2,1)S(1)} collective-permute-done((bf16[8,2176]{1,0:T(8,128)(2,1)S(1)}, bf16[8,2176]{1,0:T(8,128)(2,1)S(1)}, u32[]{:S(2)}, u32[]{:S(2)}) %collective-permute-start.134) | collective-permute-done | bytes 34848 | tf_op jit(solution)/shard_map/cond/branch_7_fun/ppermute | solution.py:336
  47.5 2.8 %away.15 = (f32[8,2048]{1,0:T(8,128)S(1)}, bf16[8,4096]{1,0:T(8,128)(2,1)S(1)}, bf16[1,4096,512]{2,1,0:T(8,128)(2,1)S(1)}) custom-call(bf16[8,2048]{1,0:T(8,128)(2,1)S(1)} %near.15, bf16[8,2176]{1,0:T(8,128)(2,1)S(1)} %collective-permute-done.134.far, f32[2,8,2048]{2,1,0:T(8,128)S(1)} %get-tuple-element.493.res, ...), custom_call_target="tpu_custom_call" | custom-call | flops 2147483648 | bytes 16777216 | tf_op jit(solution)/shard_map/cond/branch_7_fun/away/pallas_call | solution.py:445
  50.3 1.6 %collective-permute-start.135 = (f32[8,2048]{1,0:T(8,128)S(1)}, f32[8,2048]{1,0:T(8,128)S(1)}, u32[]{:S(2)}, u32[]{:S(2)}) collective-permute-start(f32[8,2048]{1,0:T(8,128)S(1)} %get-tuple-element.499), channel_id=1, source_target_pairs={{0,1},{1,0},{2,3},{3,2},{4,5},{5,4},{6,7},{7,6},{8,9},{9,8},{10,11... | collective-permute-start | bytes 196616 | tf_op jit(solution)/shard_map/cond/branch_7_fun/ppermute | solution.py:470
  51.9 2.8 %home.15 = f32[8,2048]{1,0:T(8,128)S(1)} custom-call(bf16[8,4096]{1,0:T(8,128)(2,1)S(1)} %get-tuple-element.497.attn, bf16[6,4096,512]{2,1,0:T(8,128)(2,1)S(1)} %get-tuple-element.496.w, bf16[1,4096,512]{2,1,0:T(8,128)(2,1)S(1)} %get-tuple-element.498.w_late, bf16[4096,4096]{1,0:T(8,128)(2,1)} %get-tuple-element.490.w.w_hbm), custom_call_target="tpu_custom_call" | custom-call | flops 2147483648 | bytes 16777216 | tf_op jit(solution)/shard_map/cond/branch_7_fun/home/pallas_call | solution.py:456
  54.8 0.6 %copy-done.5 = bf16[8,2048]{1,0:T(8,128)(2,1)} copy-done((bf16[8,2048]{1,0:T(8,128)(2,1)}, bf16[8,2048]{1,0:T(8,128)(2,1)S(1)}, u32[]{:S(2)}) %copy-start.5) | copy-done | bytes 32792
  (37 shorter events, 0.5 us)
Async XLA Ops:
  0.0 0.8 %copy-start = (bf16[8,4096]{1,0:T(8,128)(2,1)S(1)}, bf16[8,4096]{1,0:T(8,128)(2,1)}, u32[]{:S(2)}) copy-start(bf16[8,4096]{1,0:T(8,128)(2,1)} %q_ref.1) | copy-start | bytes 196612
  0.9 2.2 %copy-start.1 = (s32[16]{0:T(128)S(1)}, s32[16]{0:T(128)}, u32[]{:S(2)}) copy-start(s32[16]{0:T(128)} %owner_ref.1) | copy-start | bytes 196
  0.9 2.2 %copy-start.3 = (s32[1,64]{1,0:T(1,128)S(1)}, s32[1,64]{1,0:T(1,128)}, u32[]{:S(2)}) copy-start(s32[1,64]{1,0:T(1,128)} %param.28) | copy-start | bytes 772
  0.9 2.2 %copy-start.4 = (s32[8]{0:T(128)S(1)}, s32[8]{0:T(128)}, u32[]{:S(2)}) copy-start(s32[8]{0:T(128)} %param.27) | copy-start | bytes 100
  0.9 2.2 %collective-permute-start.136 = (bf16[8,2048]{1,0:T(8,128)(2,1)S(1)}, bf16[8,2048]{1,0:T(8,128)(2,1)S(1)}, u32[]{:S(2)}, u32[]{:S(2)}) collective-permute-start(bf16[8,2048]{1,0:T(8,128)(2,1)S(1)} %get-tuple-element.522.after), channel_id=1, source_target_pairs={{0,2},{2,0},{4,6},{6,4},{8,10},{10,8},{12,14},{14,12},{16,18},{18,... | collective-permute-start | bytes 98312 | tf_op jit(solution)/shard_map/ppermute | solution.py:336
  3.1 17.3 %copy-start.2 = (s32[8]{0:T(128)S(1)}, s32[8]{0:T(128)}, u32[]{:S(2)}) copy-start(s32[8]{0:T(128)} %readers.1) | copy-start | bytes 100
  3.2 17.0 %collective-permute-start.63 = (bf16[2,2048,256]{2,1,0:T(8,128)(2,1)S(1)}, bf16[2,2048,256]{2,1,0:T(8,128)(2,1)}, u32[]{:S(2)}, u32[]{:S(2)}) collective-permute-start(bf16[2,2048,256]{2,1,0:T(8,128)(2,1)S(1)} %get-tuple-element.349), channel_id=1, source_target_pairs={{0,2},{2,0},{4,6},{6,4},{8,10},{10,8},{12,14},{14,12},{16,18},{18,... | collective-permute-start | bytes 6291464 | tf_op jit(solution)/shard_map/cond/branch_7_fun/ppermute | solution.py:336
  3.3 9.0 %collective-permute-start.62 = (bf16[2,8,2048]{2,1,0:T(8,128)(2,1)S(1)}, bf16[2,8,2048]{2,1,0:T(8,128)(2,1)}, u32[]{:S(2)}, u32[]{:S(2)}) collective-permute-start(bf16[2,8,2048]{2,1,0:T(8,128)(2,1)S(1)} %get-tuple-element.348), channel_id=1, source_target_pairs={{0,28},{2,30},{4,6},{6,4},{8,10},{10,8},{12,14},{14,12},{16,18},{1... | collective-permute-start | bytes 196616 | tf_op jit(solution)/shard_map/cond/branch_7_fun/ppermute | solution.py:381
  9.3 3.1 %collective-permute-start.61 = (bf16[2,8,2048]{2,1,0:T(8,128)(2,1)S(1)}, bf16[2,8,2048]{2,1,0:T(8,128)(2,1)}, u32[]{:S(2)}, u32[]{:S(2)}) collective-permute-start(bf16[2,8,2048]{2,1,0:T(8,128)(2,1)S(1)} %get-tuple-element.348), channel_id=1, source_target_pairs={{0,2},{2,0},{4,28},{6,30},{8,10},{10,8},{12,14},{14,12},{16,18},{1... | collective-permute-start | bytes 196616 | tf_op jit(solution)/shard_map/cond/branch_7_fun/ppermute | solution.py:381
  9.3 3.6 %collective-permute-start.60 = (bf16[2,8,2048]{2,1,0:T(8,128)(2,1)S(1)}, bf16[2,8,2048]{2,1,0:T(8,128)(2,1)}, u32[]{:S(2)}, u32[]{:S(2)}) collective-permute-start(bf16[2,8,2048]{2,1,0:T(8,128)(2,1)S(1)} %get-tuple-element.348), channel_id=1, source_target_pairs={{0,2},{2,0},{4,6},{6,4},{8,28},{10,30},{12,14},{14,12},{16,18},{18... | collective-permute-start | bytes 196616 | tf_op jit(solution)/shard_map/cond/branch_7_fun/ppermute | solution.py:381
  9.8 10.4 %collective-permute-start.59 = (bf16[2,8,2048]{2,1,0:T(8,128)(2,1)S(1)}, bf16[2,8,2048]{2,1,0:T(8,128)(2,1)}, u32[]{:S(2)}, u32[]{:S(2)}) collective-permute-start(bf16[2,8,2048]{2,1,0:T(8,128)(2,1)S(1)} %get-tuple-element.348), channel_id=1, source_target_pairs={{0,2},{2,0},{4,6},{6,4},{8,10},{10,8},{12,28},{14,30},{16,18},{18,... | collective-permute-start | bytes 196616 | tf_op jit(solution)/shard_map/cond/branch_7_fun/ppermute | solution.py:381
  12.3 7.9 %collective-permute-start.58 = (bf16[2,8,2048]{2,1,0:T(8,128)(2,1)S(1)}, bf16[2,8,2048]{2,1,0:T(8,128)(2,1)}, u32[]{:S(2)}, u32[]{:S(2)}) collective-permute-start(bf16[2,8,2048]{2,1,0:T(8,128)(2,1)S(1)} %get-tuple-element.348), channel_id=1, source_target_pairs={{0,2},{2,0},{4,6},{6,4},{8,10},{10,8},{12,14},{14,12},{16,28},{18,... | collective-permute-start | bytes 196616 | tf_op jit(solution)/shard_map/cond/branch_7_fun/ppermute | solution.py:381
  12.3 7.9 %collective-permute-start.57 = (bf16[2,8,2048]{2,1,0:T(8,128)(2,1)S(1)}, bf16[2,8,2048]{2,1,0:T(8,128)(2,1)}, u32[]{:S(2)}, u32[]{:S(2)}) collective-permute-start(bf16[2,8,2048]{2,1,0:T(8,128)(2,1)S(1)} %get-tuple-element.348), channel_id=1, source_target_pairs={{0,2},{2,0},{4,6},{6,4},{8,10},{10,8},{12,14},{14,12},{16,18},{18,... | collective-permute-start | bytes 196616 | tf_op jit(solution)/shard_map/cond/branch_7_fun/ppermute | solution.py:381
  12.8 7.4 %collective-permute-start.56 = (bf16[2,8,2048]{2,1,0:T(8,128)(2,1)S(1)}, bf16[2,8,2048]{2,1,0:T(8,128)(2,1)}, u32[]{:S(2)}, u32[]{:S(2)}) collective-permute-start(bf16[2,8,2048]{2,1,0:T(8,128)(2,1)S(1)} %get-tuple-element.348), channel_id=1, source_target_pairs={{0,2},{2,0},{4,6},{6,4},{8,10},{10,8},{12,14},{14,12},{16,18},{18,... | collective-permute-start | bytes 196616 | tf_op jit(solution)/shard_map/cond/branch_7_fun/ppermute | solution.py:381
  21.4 1.5 %collective-permute-start.127 = (bf16[2,8,2176]{2,1,0:T(8,128)(2,1)S(1)}, bf16[2,8,2176]{2,1,0:T(8,128)(2,1)S(1)}, u32[]{:S(2)}, u32[]{:S(2)}) collective-permute-start(bf16[2,8,2176]{2,1,0:T(8,128)(2,1)S(1)} %get-tuple-element.483), channel_id=1, source_target_pairs={{0,2},{2,0},{4,6},{6,4},{8,10},{10,8},{12,14},{14,12},{16,18},{18,... | collective-permute-start | bytes 208904 | tf_op jit(solution)/shard_map/cond/branch_7_fun/ppermute | solution.py:381
  21.9 1.3 %collective-permute-start.128 = (bf16[2,8,2176]{2,1,0:T(8,128)(2,1)S(1)}, bf16[2,8,2176]{2,1,0:T(8,128)(2,1)S(1)}, u32[]{:S(2)}, u32[]{:S(2)}) collective-permute-start(bf16[2,8,2176]{2,1,0:T(8,128)(2,1)S(1)} %get-tuple-element.484), channel_id=1, source_target_pairs={{0,2},{2,0},{4,6},{6,4},{8,10},{10,8},{12,14},{14,12},{16,18},{18,... | collective-permute-start | bytes 208904 | tf_op jit(solution)/shard_map/cond/branch_7_fun/ppermute | solution.py:381
  21.9 24.2 %collective-permute-start.129 = (bf16[2,8,2176]{2,1,0:T(8,128)(2,1)S(1)}, bf16[2,8,2176]{2,1,0:T(8,128)(2,1)S(1)}, u32[]{:S(2)}, u32[]{:S(2)}) collective-permute-start(bf16[2,8,2176]{2,1,0:T(8,128)(2,1)S(1)} %get-tuple-element.485), channel_id=1, source_target_pairs={{0,2},{2,0},{4,6},{6,4},{8,10},{10,8},{12,14},{14,12},{16,28},{18,... | collective-permute-start | bytes 208904 | tf_op jit(solution)/shard_map/cond/branch_7_fun/ppermute | solution.py:381
  22.4 23.8 %collective-permute-start.130 = (bf16[2,8,2176]{2,1,0:T(8,128)(2,1)S(1)}, bf16[2,8,2176]{2,1,0:T(8,128)(2,1)S(1)}, u32[]{:S(2)}, u32[]{:S(2)}) collective-permute-start(bf16[2,8,2176]{2,1,0:T(8,128)(2,1)S(1)} %get-tuple-element.486), channel_id=1, source_target_pairs={{0,2},{2,0},{4,6},{6,4},{8,10},{10,8},{12,28},{14,30},{16,18},{18,... | collective-permute-start | bytes 208904 | tf_op jit(solution)/shard_map/cond/branch_7_fun/ppermute | solution.py:381
  22.5 23.7 %collective-permute-start.131 = (bf16[2,8,2176]{2,1,0:T(8,128)(2,1)S(1)}, bf16[2,8,2176]{2,1,0:T(8,128)(2,1)S(1)}, u32[]{:S(2)}, u32[]{:S(2)}) collective-permute-start(bf16[2,8,2176]{2,1,0:T(8,128)(2,1)S(1)} %get-tuple-element.487), channel_id=1, source_target_pairs={{0,2},{2,0},{4,6},{6,4},{8,28},{10,30},{12,14},{14,12},{16,18},{18... | collective-permute-start | bytes 208904 | tf_op jit(solution)/shard_map/cond/branch_7_fun/ppermute | solution.py:381
  22.9 23.3 %collective-permute-start.132 = (bf16[2,8,2176]{2,1,0:T(8,128)(2,1)S(1)}, bf16[2,8,2176]{2,1,0:T(8,128)(2,1)S(1)}, u32[]{:S(2)}, u32[]{:S(2)}) collective-permute-start(bf16[2,8,2176]{2,1,0:T(8,128)(2,1)S(1)} %get-tuple-element.488), channel_id=1, source_target_pairs={{0,2},{2,0},{4,28},{6,30},{8,10},{10,8},{12,14},{14,12},{16,18},{1... | collective-permute-start | bytes 208904 | tf_op jit(solution)/shard_map/cond/branch_7_fun/ppermute | solution.py:381
  23.1 23.0 %collective-permute-start.133 = (bf16[2,8,2176]{2,1,0:T(8,128)(2,1)S(1)}, bf16[2,8,2176]{2,1,0:T(8,128)(2,1)S(1)}, u32[]{:S(2)}, u32[]{:S(2)}) collective-permute-start(bf16[2,8,2176]{2,1,0:T(8,128)(2,1)S(1)} %get-tuple-element.489), channel_id=1, source_target_pairs={{0,28},{2,30},{4,6},{6,4},{8,10},{10,8},{12,14},{14,12},{16,18},{1... | collective-permute-start | bytes 208904 | tf_op jit(solution)/shard_map/cond/branch_7_fun/ppermute | solution.py:381
  46.2 1.3 %collective-permute-start.134 = (bf16[8,2176]{1,0:T(8,128)(2,1)S(1)}, bf16[8,2176]{1,0:T(8,128)(2,1)S(1)}, u32[]{:S(2)}, u32[]{:S(2)}) collective-permute-start(bf16[8,2176]{1,0:T(8,128)(2,1)S(1)} %get-tuple-element.495), channel_id=1, source_target_pairs={{0,2},{2,0},{4,6},{6,4},{8,10},{10,8},{12,14},{14,12},{16,18},{18,... | collective-permute-start | bytes 104456 | tf_op jit(solution)/shard_map/cond/branch_7_fun/ppermute | solution.py:336
  50.3 4.5 %collective-permute-start.135 = (f32[8,2048]{1,0:T(8,128)S(1)}, f32[8,2048]{1,0:T(8,128)S(1)}, u32[]{:S(2)}, u32[]{:S(2)}) collective-permute-start(f32[8,2048]{1,0:T(8,128)S(1)} %get-tuple-element.499), channel_id=1, source_target_pairs={{0,1},{1,0},{2,3},{3,2},{4,5},{5,4},{6,7},{7,6},{8,9},{9,8},{10,11... | collective-permute-start | bytes 196616 | tf_op jit(solution)/shard_map/cond/branch_7_fun/ppermute | solution.py:470
  54.8 0.6 %copy-start.5 = (bf16[8,2048]{1,0:T(8,128)(2,1)}, bf16[8,2048]{1,0:T(8,128)(2,1)S(1)}, u32[]{:S(2)}) copy-start(bf16[8,2048]{1,0:T(8,128)(2,1)S(1)} %get-tuple-element.787) | copy-start | bytes 98308
